TPU v7x, 32 devices: a whole 2x2x4 slice. The times are simulated.
32 devices in a mesh: gx: 16 (over z, y, x), gz: 2 (over core).
Axes of the slice: x: 2, y: 2, z: 4, core: 2. Of those that a mesh axis runs over, the one named last changes fastest.
Arguments:
- velocity: float32 [3, 256, 16, 256], P(None, 'gx', 'gz'), may hold values from -6 to 6
- pressure: float32 [256, 16, 256], P('gx', 'gz'), may hold values from 1 to 3
- stress_old: float32 [6, 256, 16, 256], P(None, 'gx', 'gz'), may hold values from -6 to 6
- plastic: float32 [256, 16, 256], P('gx', 'gz'), may hold values from 0 to 2
- viscosity: float32 [256, 16, 256], P('gx', 'gz'), may hold values from 1 to 30
- weak_seed: int32 [256, 16, 256], P('gx', 'gz'), may hold values 0 or 1
Outputs:
- velocity_out: float32 [3, 256, 16, 256], P(None, 'gx', 'gz')
- pressure_out: float32 [256, 16, 256], P('gx', 'gz')
- stress_out: float32 [6, 256, 16, 256], P(None, 'gx', 'gz')
- plastic_out: float32 [256, 16, 256], P('gx', 'gz')
- yield_peak: float32 [2], replicated
All inputs are finite; a program needn't handle non-finite values. No bound on the sum of `weak_seed` on one device may be relied on, other than what follows from the above.
Results may differ from a plain program's by a relative error of at most 0.000059.
Values sent between devices are 32-bit elements; how exact they have to be, the bound alone decides.
A program may use at most 64 MiB of HBM per device.

v0:
```python
import functools
import math

import jax
import jax.numpy as jnp
from jax import lax
from jax.experimental import pallas as pl
from jax.experimental.pallas import tpu as pltpu
from jax.sharding import PartitionSpec as P

ITERS = 2
REACH = 6
BLOCK = 2
UNROLL = 1
MESH = pl.DeviceIdType.MESH

unnormalized_weights = [math.exp(-(k * k) / 18.0) for k in range(-REACH, REACH + 1)]
weight_total = sum(unnormalized_weights)
gauss_weights = [value / weight_total for value in unnormalized_weights]
shear_time_increment = 20.0


def kernel(
    gx_count,
    gz_count,
    vel_in,
    pres_in,
    old_in,
    plas_in,
    visc_in,
    weak_in,
    VOUT,
    PR,
    TAU,
    PL,
    peak_out,
    V,
    PIN,
    OLD,
    PLX,
    VI,
    WK,
    ETA,
    COH,
    YM,
    GX,
    GZH,
    SM,
    VZE,
    VZH,
    SX,
    TZ,
    SZE,
    SZH,
    RP,
    RH,
    R,
    RZE,
    RZH,
    TB,
    PK,
    in_sem,
    send_sem,
    recv_sem,
    pk_send,
    pk_recv,
):
    rows, nz, ny = PR.shape
    gx = lax.axis_index("gx")
    gz = lax.axis_index("gz")
    me = gx * gz_count + gz
    total = gx_count * gz_count
    has = {
        "xl": gx > 0,
        "xh": gx < gx_count - 1,
        "zl": gz > 0,
        "zh": gz < gz_count - 1,
    }
    target = {
        "xl": (gx - 1, gz),
        "xh": (gx + 1, gz),
        "zl": (gx, gz - 1),
        "zh": (gx, gz + 1),
    }
    opposite = {"xl": "xh", "xh": "xl", "zl": "zh", "zh": "zl"}

    barrier = pltpu.get_barrier_semaphore()

    def to_others(act):
        for dz_ in range(gz_count):
            other_z = gz + dz_
            other_z = jnp.where(other_z >= gz_count, other_z - gz_count, other_z)

            def body(dx_, carry):
                other_x = gx + dx_
                act((jnp.where(other_x >= gx_count, other_x - gx_count, other_x), other_z))
                return carry

            lax.fori_loop(0 if dz_ else 1, gx_count, body, 0, unroll=UNROLL)

    loads = [
        pltpu.make_async_copy(plas_in, PLX.at[pl.ds(REACH, rows)], in_sem.at[0]),
        pltpu.make_async_copy(vel_in, V.at[:, pl.ds(1, rows)], in_sem.at[1]),
        pltpu.make_async_copy(visc_in, VI, in_sem.at[2]),
        pltpu.make_async_copy(weak_in, WK, in_sem.at[3]),
        pltpu.make_async_copy(old_in, OLD, in_sem.at[4]),
        pltpu.make_async_copy(pres_in, PIN, in_sem.at[5]),
    ]
    for copy in loads[:2]:
        copy.start()
    to_others(
        lambda place: pl.semaphore_signal(
            barrier, inc=1, device_id=place, device_id_type=MESH
        )
    )
    for copy in loads[2:]:
        copy.start()

    count = [0]

    def exchange(side, source, landing):
        slot = count[0]
        count[0] += 1
        copy = pltpu.make_async_remote_copy(
            src_ref=source,
            dst_ref=landing,
            send_sem=send_sem.at[slot],
            recv_sem=recv_sem.at[slot],
            device_id=target[side],
            device_id_type=MESH,
        )

        @pl.when(has[side])
        def _():
            copy.start()

        return side, copy

    def wait_sent(pair):
        side, copy = pair

        @pl.when(has[side])
        def _():
            copy.wait_send()

    def wait_got(pair):
        side, copy = pair

        @pl.when(has[opposite[side]])
        def _():
            copy.wait_recv()

    def zero_unless(side, ref):
        @pl.when(jnp.logical_not(has[side]))
        def _():
            ref[...] = jnp.zeros(ref.shape, ref.dtype)

    zero_unless("xl", PLX.at[pl.ds(0, REACH)])
    zero_unless("xh", PLX.at[pl.ds(rows + REACH, REACH)])
    zero_unless("xl", V.at[:, pl.ds(0, 1)])
    zero_unless("xh", V.at[:, pl.ds(rows + 1, 1)])
    zero_unless("zl", GZH.at[0])
    zero_unless("zh", GZH.at[1])
    for buf in (VZH.at[0], RZH.at[0], SZH.at[0, 0], SZH.at[1, 0]):
        zero_unless("zl", buf)
    for buf in (VZH.at[1], RZH.at[1], SZH.at[0, 1], SZH.at[1, 1]):
        zero_unless("zh", buf)
    for it in range(ITERS):
        zero_unless("xl", SX.at[it, :, pl.ds(0, 1)])
        zero_unless("xh", SX.at[it, :, pl.ds(rows + 1, 1)])

    loads[0].wait()
    loads[1].wait()

    def vel_edges(x, carry):
        for c in range(3):
            row = V[c, x + 1]
            VZE[0, c, x] = row[0:1]
            VZE[1, c, x] = row[nz - 1 : nz]
        return carry

    lax.fori_loop(0, rows, vel_edges, 0)
    pl.semaphore_wait(barrier, total - 1)
    plas_copies = [
        exchange("xh", PLX.at[pl.ds(rows, REACH)], PLX.at[pl.ds(0, REACH)]),
        exchange("xl", PLX.at[pl.ds(REACH, REACH)], PLX.at[pl.ds(rows + REACH, REACH)]),
    ]
    vel_copies = [
        exchange("xh", V.at[:, pl.ds(rows, 1)], V.at[:, pl.ds(0, 1)]),
        exchange("xl", V.at[:, pl.ds(1, 1)], V.at[:, pl.ds(rows + 1, 1)]),
    ]

    vz_copies = [
        exchange("zh", VZE.at[1], VZH.at[0]),
        exchange("zl", VZE.at[0], VZH.at[1]),
    ]

    places_a = lax.broadcasted_iota(jnp.int32, (ny, ny), 0)
    places_b = lax.broadcasted_iota(jnp.int32, (ny, ny), 1)
    gap = (places_a - places_b).astype(jnp.float32)
    YM[...] = jnp.where(
        jnp.abs(gap) <= float(REACH), jnp.exp(-gap * gap / 18.0) / weight_total, 0.0
    )
    for copy in loads[2:]:
        copy.wait()

    def prepare(x, carry):
        eta = VI[x]
        ETA[x] = shear_time_increment * eta / (eta + shear_time_increment)
        return carry

    lax.fori_loop(0, rows, prepare, 0)

    block = next(size for size in (BLOCK, 2, 1) if rows % size == 0)
    many = (block, nz, ny)
    sub = lax.broadcasted_iota(jnp.int32, many, 1)
    lane = lax.broadcasted_iota(jnp.int32, many, 2)

    def over_rows(body, carry=0):
        return lax.fori_loop(0, rows // block, lambda i, state: body(i * block, state), carry)

    def at(x):
        return pl.ds(x, block)

    for pair in plas_copies:
        wait_got(pair)

    def smooth_x(x, carry):
        sum_ = gauss_weights[REACH] * PLX[at(x + REACH)]
        for k in range(1, REACH + 1):
            sum_ = sum_ + gauss_weights[REACH + k] * (PLX[at(x + REACH - k)] + PLX[at(x + REACH + k)])
        GX[at(x)] = sum_
        return carry

    over_rows(smooth_x)
    gz_copies = [
        exchange("zh", GX, GZH.at[0]),
        exchange("zl", GX, GZH.at[1]),
    ]
    for pair in vel_copies + vz_copies:
        wait_got(pair)

    def dy(f):
        up = jnp.where(lane < ny - 1, pltpu.roll(f, ny - 1, 2), 0.0)
        down = jnp.where(lane > 0, pltpu.roll(f, 1, 2), 0.0)
        return (up - down) * 0.5

    def dz(f, low, high):
        up = pltpu.roll(jnp.where(sub >= 1, f, jnp.broadcast_to(high, f.shape)), nz - 1, 1)
        down = pltpu.roll(jnp.where(sub < nz - 1, f, jnp.broadcast_to(low, f.shape)), 1, 1)
        return (up - down) * 0.5

    def trial_stress(x, pres):
        v = [V[c, at(x + 1)] for c in range(3)]
        dx_v = [(V[c, at(x + 2)] - V[c, at(x)]) * 0.5 for c in range(3)]
        dz_v = [dz(f, VZH[0, c, at(x)], VZH[1, c, at(x)]) for c, f in enumerate(v)]
        dy_v = [dy(f) for f in v]
        div = dx_v[0] + dz_v[1] + dy_v[2]
        third = div * (1.0 / 3.0)
        pres = pres - 0.25 * div
        PR[at(x)] = pres
        strain = (
            dx_v[0] - third,
            dz_v[1] - third,
            dy_v[2] - third,
            0.5 * (dx_v[1] + dz_v[0]),
            0.5 * (dx_v[2] + dy_v[0]),
            0.5 * (dz_v[2] + dy_v[1]),
        )
        twice = 2.0 * ETA[at(x)]
        trial = [
            twice * (strain[c] + OLD[c, at(x)] * (0.5 / shear_time_increment)) for c in range(6)
        ]
        tau_ii = jnp.sqrt(
            0.5 * (trial[0] * trial[0] + trial[1] * trial[1] + trial[2] * trial[2])
            + trial[3] * trial[3]
            + trial[4] * trial[4]
            + trial[5] * trial[5]
        )
        return pres, trial, tau_ii

    def first_trial(x, carry):
        _, trial, tau_ii = trial_stress(x, PIN[at(x)])
        for c in range(6):
            TAU[c, at(x)] = trial[c]
        TB[at(x)] = tau_ii
        return carry

    over_rows(first_trial)

    for pair in gz_copies:
        wait_got(pair)

    def smooth_z(x, carry):
        own, low, high = GX[at(x)], GZH[0, at(x)], GZH[1, at(x)]
        sum_ = gauss_weights[REACH] * own
        for k in range(1, REACH + 1):
            above = pltpu.roll(jnp.where(sub >= k, own, high), nz - k, 1)
            below = pltpu.roll(jnp.where(sub < nz - k, own, low), k, 1)
            sum_ = sum_ + gauss_weights[REACH + k] * (above + below)
        SM[at(x)] = sum_
        return carry

    over_rows(smooth_z)
    SM[...] = jnp.dot(
        SM[...].reshape(rows * nz, ny),
        YM[...],
        precision=lax.Precision.HIGHEST,
        preferred_element_type=jnp.float32,
    ).reshape(rows, nz, ny)

    half = ny // 2 if ny % 256 == 0 else ny
    tops = []
    for it in range(ITERS):
        last = it == ITERS - 1

        def stress_row(x, carry, it=it, last=last):
            most_f, most_eta = carry
            if it == 0:
                pres, trial, tau_ii = PR[at(x)], [TAU[c, at(x)] for c in range(6)], TB[at(x)]
                seeded = WK[at(x)].astype(jnp.float32)
                strength = 0.8660254 * ((1.0 - 0.6 * seeded) / (1.0 + 2.0 * SM[at(x)]))
                COH[at(x)] = strength
                plas = PLX[at(x + REACH)]
            else:
                pres, trial, tau_ii = trial_stress(x, PR[at(x)])
                strength = COH[at(x)]
                plas = PL[at(x)]
            eta = ETA[at(x)]
            yield_f = tau_ii - 0.5 * jnp.maximum(pres, 0.0) - strength
            dlam = jnp.maximum(yield_f, 0.0) / (eta + 0.5)
            shrink = 1.0 - eta * dlam / jnp.maximum(tau_ii, 0.5)
            tau = [shrink * value for value in trial]
            PL[at(x)] = plas + dlam
            if last:
                for c in range(6):
                    TAU[c, at(x)] = tau[c]
            SX[it, 0, at(x + 1)] = tau[0] - pres
            SX[it, 1, at(x + 1)] = tau[3]
            SX[it, 2, at(x + 1)] = tau[4]
            szz = tau[1] - pres
            TZ[0, at(x)] = szz
            TZ[1, at(x)] = tau[5]
            TZ[2, at(x)] = tau[2] - pres
            for c, f in enumerate((tau[3], szz, tau[5])):
                SZE[it, 0, c, at(x)] = f[:, 0:1]
                SZE[it, 1, c, at(x)] = f[:, nz - 1 : nz]
            return jnp.maximum(most_f, yield_f), jnp.maximum(most_eta, eta * shrink)

        start = jnp.full(many, -jnp.inf, jnp.float32)
        most_f, most_eta = over_rows(stress_row, (start, start))
        sx_copies = [
            exchange("xh", SX.at[it, :, pl.ds(rows, 1)], SX.at[it, :, pl.ds(0, 1)]),
            exchange("xl", SX.at[it, :, pl.ds(1, 1)], SX.at[it, :, pl.ds(rows + 1, 1)]),
        ]
        sz_copies = [
            exchange("zh", SZE.at[it, 1], SZH.at[it, 0]),
            exchange("zl", SZE.at[it, 0], SZH.at[it, 1]),
        ]

        def folded(most):
            most = jnp.max(jnp.max(most, axis=0), axis=0, keepdims=True)
            return jnp.maximum(most[:, :half], most[:, ny - half :])

        PK[it, me] = jnp.concatenate([folded(most_f), folded(most_eta)], axis=0)

        def tell(place, it=it):
            pltpu.make_async_remote_copy(
                src_ref=PK.at[it, me],
                dst_ref=PK.at[it, me],
                send_sem=pk_send.at[it],
                recv_sem=pk_recv.at[it],
                device_id=place,
                device_id_type=MESH,
            ).start()

        to_others(tell)
        for pair in sz_copies:
            wait_got(pair)

        def inner_row(x, carry, it=it):
            txz, txy = SX[it, 1, at(x + 1)], SX[it, 2, at(x + 1)]
            szz, tzy, syy = TZ[0, at(x)], TZ[1, at(x)], TZ[2, at(x)]
            z_terms = [
                dz(f, SZH[it, 0, c, at(x)], SZH[it, 1, c, at(x)])
                for c, f in enumerate((txz, szz, tzy))
            ]
            y_terms = [dy(f) for f in (txy, tzy, syy)]
            for c in range(3):
                R[c, at(x)] = z_terms[c] + y_terms[c]
            return carry

        def add_x(low, high, it=it):
            for c in range(3):
                R[c, low:high] = R[c, low:high] + 0.5 * (
                    SX[it, c, low + 2 : high + 2] - SX[it, c, low:high]
                )

        r_copies = []
        if not last:
            inner_row(0, 0)
            inner_row(rows - block, 0)
            for c in range(3):
                RP[0, c] = R[c, 0] + 0.5 * SX[it, c, 2]
                RP[1, c] = R[c, rows - 1] - 0.5 * SX[it, c, rows - 1]
            r_copies += [
                exchange("xh", RP.at[1], RH.at[0]),
                exchange("xl", RP.at[0], RH.at[1]),
            ]
        over_rows(inner_row)
        add_x(1, rows - 1)
        for pair in sx_copies:
            wait_got(pair)
        add_x(0, 1)
        add_x(rows - 1, rows)
        if not last:

            def edges(x, carry):
                for c in range(3):
                    value = R[c, at(x)]
                    RZE[0, c, at(x)] = value[:, 0:1]
                    RZE[1, c, at(x)] = value[:, nz - 1 : nz]
                return carry

            over_rows(edges)
            r_copies += [
                exchange("zh", RZE.at[1], RZH.at[0]),
                exchange("zl", RZE.at[0], RZH.at[1]),
            ]
            for pair in vel_copies:
                wait_sent(pair)
            for pair in r_copies:
                wait_got(pair)

        others = PK.at[it, pl.ds(0, total - 1)]
        arrived = pltpu.make_async_copy(others, others, pk_recv.at[it])
        arrived.wait()
        peaks = jnp.max(PK[it], axis=0)
        step = 0.125 / jnp.max(peaks[1:2], axis=1, keepdims=True)

        def velocity_row(x, carry):
            for c in range(3):
                value = V[c, at(x + 1)] + step * R[c, at(x)]
                if last:
                    VOUT[c, at(x)] = value
                else:
                    V[c, at(x + 1)] = value
            return carry

        over_rows(velocity_row)
        if not last:

            @pl.when(has["xl"])
            def _(it=it, step=step):
                for c in range(3):
                    V[c, 0] = V[c, 0] + step * (RH[0, c] + 0.5 * SX[it, c, 1])

            @pl.when(has["xh"])
            def _(it=it, step=step):
                for c in range(3):
                    V[c, rows + 1] = V[c, rows + 1] + step * (RH[1, c] - 0.5 * SX[it, c, rows])

            VZH[...] = VZH[...] + step * RZH[...]
        tops.append(jnp.max(peaks[0:1], axis=1, keepdims=True))
        for pair in sx_copies + sz_copies + r_copies:
            wait_sent(pair)
        pltpu.make_async_copy(others, others, pk_send.at[it]).wait()

    peak_out[...] = jnp.concatenate(tops, axis=1)[0]
    for pair in plas_copies + vz_copies + gz_copies:
        wait_sent(pair)


def store_kernel(*refs):
    held, out, sem = refs[:5], refs[5:10], refs[10]
    copies = [pltpu.make_async_copy(a, b, sem.at[i]) for i, (a, b) in enumerate(zip(held, out))]
    for copy in copies:
        copy.start()
    for copy in copies:
        copy.wait()


def solution(mesh):
    gx_count, gz_count = mesh.shape["gx"], mesh.shape["gz"]
    total = gx_count * gz_count

    def per_device(velocity, pressure, stress_old, plastic, viscosity, weak_seed):
        rows, nz, ny = pressure.shape
        cells = (rows, nz, ny)
        f32 = jnp.float32
        vm = lambda *shape: pltpu.VMEM(shape, f32)
        copies = 6 + 2 + 4 * ITERS + 4 * (ITERS - 1)
        anywhere = pl.BlockSpec(memory_space=pl.ANY)
        shapes = (velocity.shape, pressure.shape, stress_old.shape, plastic.shape)
        held = pl.pallas_call(
            functools.partial(kernel, gx_count, gz_count),
            out_shape=tuple(vm(*shape) for shape in shapes + ((ITERS,),)),
            in_specs=[anywhere] * 6,
            out_specs=(pl.BlockSpec(memory_space=pltpu.VMEM),) * 5,
            scratch_shapes=[
                vm(3, rows + 2, nz, ny),
                vm(*cells),
                vm(6, *cells),
                vm(rows + 2 * REACH, nz, ny),
                vm(*cells),
                pltpu.VMEM(cells, jnp.int32),
                vm(*cells),
                vm(*cells),
                vm(ny, ny),
                vm(*cells),
                vm(2, *cells),
                vm(*cells),
                vm(2, 3, rows, 1, ny),
                vm(2, 3, rows, 1, ny),
                vm(ITERS, 3, rows + 2, nz, ny),
                vm(3, *cells),
                vm(ITERS, 2, 3, rows, 1, ny),
                vm(ITERS, 2, 3, rows, 1, ny),
                vm(2, 3, nz, ny),
                vm(2, 3, nz, ny),
                vm(3, *cells),
                vm(2, 3, rows, 1, ny),
                vm(2, 3, rows, 1, ny),
                vm(*cells),
                vm(ITERS, total, 2, ny // 2 if ny % 256 == 0 else ny),
                pltpu.SemaphoreType.DMA((6,)),
                pltpu.SemaphoreType.DMA((copies,)),
                pltpu.SemaphoreType.DMA((copies,)),
                pltpu.SemaphoreType.DMA((ITERS,)),
                pltpu.SemaphoreType.DMA((ITERS,)),
            ],
            compiler_params=pltpu.CompilerParams(collective_id=0, has_side_effects=True),
        )(velocity, pressure, stress_old, plastic, viscosity, weak_seed)
        held = [pltpu.with_memory_space_constraint(array, pltpu.VMEM) for array in held]
        return pl.pallas_call(
            store_kernel,
            out_shape=tuple(jax.ShapeDtypeStruct(shape, f32) for shape in shapes)
            + (jax.ShapeDtypeStruct((ITERS,), f32),),
            in_specs=[anywhere] * 5,
            out_specs=(anywhere,) * 5,
            scratch_shapes=[pltpu.SemaphoreType.DMA((5,))],
        )(*held)

    in_specs = (
        P(None, "gx", "gz", None),
        P("gx", "gz", None),
        P(None, "gx", "gz", None),
        P("gx", "gz", None),
        P("gx", "gz", None),
        P("gx", "gz", None),
    )
    out_specs = (
        P(None, "gx", "gz", None),
        P("gx", "gz", None),
        P(None, "gx", "gz", None),
        P("gx", "gz", None),
        P(),
    )
    return jax.shard_map(
        per_device, mesh=mesh, in_specs=in_specs, out_specs=out_specs, check_vma=False
    )
```

profile of v0, /device:TPU:0, one launch (start us, length us, event | category | flops | bytes accessed | tf_op | source)
XLA Modules:
  0.0 26.5 jit_solution(13160992501424491210)
XLA Ops:
  0.6 24.7 %shard_map.101 = (f32[3,16,8,256]{3,2,1,0:T(8,128)S(1)}, f32[16,8,256]{2,1,0:T(8,128)S(1)}, f32[6,16,8,256]{3,2,1,0:T(8,128)S(1)}, f32[16,8,256]{2,1,0:T(8,128)S(1)}, f32[2]{0:T(128)S(1)}) custom-call(f32[3,16,8,256]{3,2,1,0:T(8,128)} %vel_in.1, f32[16,8,256]{2,1,0:T(8,128)} %pres_in.1, f32[6,16,8,256]{3,2,1,0:T(8,128)} %old_in.1, f32[16,8,256]{2,1,0:T(8,128)} %plas_in.1, ...), custom_call_target="tpu_custom_call" | custom-call | tf_op jit(solution)/shard_map/pallas_call | solution.py:495
  25.4 1.1 %shard_map.102 = (f32[3,16,8,256]{3,2,1,0:T(8,128)}, f32[16,8,256]{2,1,0:T(8,128)}, f32[6,16,8,256]{3,2,1,0:T(8,128)}, f32[16,8,256]{2,1,0:T(8,128)}, f32[2]{0:T(128)}) custom-call(f32[3,16,8,256]{3,2,1,0:T(8,128)S(1)} %get-tuple-element.10.refs_0_, f32[16,8,256]{2,1,0:T(8,128)S(1)} %get-tuple-element.11.refs_1_, ...), custom_call_target="tpu_custom_call" | custom-call | tf_op jit(solution)/shard_map/pallas_call | solution.py:535
where the time goes:
time: 26.7 us; the launch traced here: 26.5 us
  Pallas kernels  25.9 us (97%)
  between operations  0.64 us (2%)
    pallas_call x1, Pallas kernels, per_device(): pl.pallas_call(functools.partial(kernel, gx_count, gz_count), out_shape=t...  24.7 us
    pallas_call x1, Pallas kernels, per_device(): pl.pallas_call(store_kernel, out_shape=tuple((jax.ShapeDtypeStruct(shape,...  1.14 us

commit v1 on v0

--- a/solution.py
+++ b/solution.py
@@ -10,7 +10,7 @@
 
 ITERS = 2
 REACH = 6
-BLOCK = 2
+BLOCK = 8
 UNROLL = 1
 MESH = pl.DeviceIdType.MESH
 
@@ -211,7 +211,7 @@
 
     lax.fori_loop(0, rows, prepare, 0)
 
-    block = next(size for size in (BLOCK, 2, 1) if rows % size == 0)
+    block = next(size for size in (BLOCK, 4, 2, 1) if rows % size == 0)
     many = (block, nz, ny)
     sub = lax.broadcasted_iota(jnp.int32, many, 1)
     lane = lax.broadcasted_iota(jnp.int32, many, 2)

time: 26.7 us -> 25.8 us (0.966)
  Pallas kernels: 25.9 us -> 25 us
    pallas_call x1, Pallas kernels: 24.7 us -> 23.9 us  [per_device(): pl.pallas_call(functools.partial(kernel, gx_count, gz_count), out_shape=t...]
where the time goes in v1:
time: 25.8 us; the launch traced here: 25.7 us
  Pallas kernels  25 us (97%)
  between operations  0.64 us (2%)
    pallas_call x1, Pallas kernels, per_device(): pl.pallas_call(functools.partial(kernel, gx_count, gz_count), out_shape=t...  23.9 us
    pallas_call x1, Pallas kernels, per_device(): pl.pallas_call(store_kernel, out_shape=tuple((jax.ShapeDtypeStruct(shape,...  1.14 us

profile of v1, /device:TPU:0, one launch (start us, length us, event | category | flops | bytes accessed | tf_op | source)
XLA Modules:
  0.0 25.7 jit_solution(8154928154649038603)
XLA Ops:
  0.6 23.9 %shard_map.101 = (f32[3,16,8,256]{3,2,1,0:T(8,128)S(1)}, f32[16,8,256]{2,1,0:T(8,128)S(1)}, f32[6,16,8,256]{3,2,1,0:T(8,128)S(1)}, f32[16,8,256]{2,1,0:T(8,128)S(1)}, f32[2]{0:T(128)S(1)}) custom-call(f32[3,16,8,256]{3,2,1,0:T(8,128)} %vel_in.1, f32[16,8,256]{2,1,0:T(8,128)} %pres_in.1, f32[6,16,8,256]{3,2,1,0:T(8,128)} %old_in.1, f32[16,8,256]{2,1,0:T(8,128)} %plas_in.1, ...), custom_call_target="tpu_custom_call" | custom-call | tf_op jit(solution)/shard_map/pallas_call | solution.py:495
  24.5 1.1 %shard_map.102 = (f32[3,16,8,256]{3,2,1,0:T(8,128)}, f32[16,8,256]{2,1,0:T(8,128)}, f32[6,16,8,256]{3,2,1,0:T(8,128)}, f32[16,8,256]{2,1,0:T(8,128)}, f32[2]{0:T(128)}) custom-call(f32[3,16,8,256]{3,2,1,0:T(8,128)S(1)} %get-tuple-element.10.refs_0_, f32[16,8,256]{2,1,0:T(8,128)S(1)} %get-tuple-element.11.refs_1_, ...), custom_call_target="tpu_custom_call" | custom-call | tf_op jit(solution)/shard_map/pallas_call | solution.py:535

commit v2 on v1

v2 whole, which is shorter than its diff:
```python
import functools
import math

import jax
import jax.numpy as jnp
from jax import lax
from jax.experimental import pallas as pl
from jax.experimental.pallas import tpu as pltpu
from jax.sharding import PartitionSpec as P

ITERS = 2
REACH = 6
BLOCK = 8
PLANE = 4
MESH = pl.DeviceIdType.MESH

unnormalized_weights = [math.exp(-(k * k) / 18.0) for k in range(-REACH, REACH + 1)]
weight_total = sum(unnormalized_weights)
gauss_weights = [value / weight_total for value in unnormalized_weights]
shear_time_increment = 20.0


def bits_of(count):
    assert count & (count - 1) == 0
    return [1 << bit for bit in range(count.bit_length() - 1)]


def kernel(
    gx_count,
    gz_count,
    vel_in,
    pres_in,
    old_in,
    plas_in,
    visc_in,
    weak_in,
    VOUT,
    PR,
    TAU,
    PL,
    peak_out,
    V,
    IN,
    WK,
    PLZ,
    PZH,
    ETA,
    INV,
    COH,
    YM,
    GX,
    GXH,
    SM,
    VZE,
    VZH,
    SX,
    TZ,
    SE,
    ZH,
    XS,
    XH,
    CE,
    CH,
    SEL,
    ZHL,
    XHL,
    RF,
    RZF,
    TR,
    DV,
    TB,
    PK,
    in_sem,
    send_sem,
    recv_sem,
    pk_send,
    pk_recv,
    pair_sem,
    hop_sem,
):
    rows, nz, ny = PR.shape
    gx = lax.axis_index("gx")
    gz = lax.axis_index("gz")
    me = gx * gz_count + gz
    total = gx_count * gz_count
    has = {
        "xl": gx > 0,
        "xh": gx < gx_count - 1,
        "zl": gz > 0,
        "zh": gz < gz_count - 1,
    }
    target = {
        "xl": (gx - 1, gz),
        "xh": (gx + 1, gz),
        "zl": (gx, gz - 1),
        "zh": (gx, gz + 1),
    }
    opposite = {"xl": "xh", "xh": "xl", "zl": "zh", "zh": "zl"}
    corners = [(a, b) for a in ("xl", "xh") for b in ("zl", "zh")]
    for a, b in corners:
        has[a + b] = jnp.logical_and(has[a], has[b])
        target[a + b] = (target[a][0], target[b][1])
        opposite[a + b] = opposite[a] + opposite[b]
    barrier = pltpu.get_barrier_semaphore()

    side_of = gz % 2
    odd = side_of == 1
    even = side_of == 0
    lead = gz + 1 - side_of
    couple = gz // 2

    def flipped(index, bit):
        return index + bit * (1 - 2 * ((index // bit) % 2))

    always = gx >= 0
    rounds = [[(flipped(gx, bit), gz, always)] for bit in bits_of(min(PLANE, gx_count))]
    rounds += [
        [(gx - far, gz, gx >= far), (gx + far, gz, gx < gx_count - far)]
        for far in bits_of(gx_count)
        if far >= PLANE
    ]
    rounds += [[(gx, 2 * flipped(couple, bit) + 1, always)] for bit in bits_of(gz_count // 2)]
    along_gx = len(bits_of(gx_count))
    met = [place for far in rounds[1:3] + rounds[max(along_gx, 3) :] for place in far]

    def signal(sem, place):
        pl.semaphore_signal(sem, inc=1, device_id=place, device_id_type=MESH)

    def one_if(flag):
        return jnp.where(flag, 1, 0)

    VI, PIN = IN.at[0], IN.at[1]
    plas_load = pltpu.make_async_copy(plas_in, PLZ, in_sem.at[0])
    vel_load = pltpu.make_async_copy(vel_in, V.at[:, pl.ds(1, rows)], in_sem.at[1])
    weak_load = pltpu.make_async_copy(weak_in, WK, in_sem.at[2])
    rest_loads = [
        pltpu.make_async_copy(visc_in, VI, in_sem.at[3]),
        pltpu.make_async_copy(pres_in, PIN, in_sem.at[3]),
        pltpu.make_async_copy(old_in, IN.at[pl.ds(2, 6)], in_sem.at[3]),
    ]
    all_rest = pltpu.make_async_copy(IN, IN, in_sem.at[3])

    @pl.when(odd)
    def _():
        signal(barrier, (gx, gz - 1))

        @pl.when(has["zh"])
        def _():
            signal(barrier, (gx, gz + 1))

    for side in ("xl", "xh"):

        @pl.when(has[side])
        def _(side=side):
            signal(barrier, (target[side][0], lead))

    plas_load.start()

    @pl.when(odd)
    def _():
        for x_place, z_place, there in met:

            @pl.when(there)
            def _(x_place=x_place, z_place=z_place):
                signal(barrier, (x_place, z_place))

    def described(side, source, landing, got, sent):
        number = {"xl": 0, "xh": 1, "zl": 0, "zh": 1}.get(side, 0)
        return pltpu.make_async_remote_copy(
            src_ref=source,
            dst_ref=landing,
            send_sem=send_sem.at[2 * sent + number],
            recv_sem=recv_sem.at[2 * got + number],
            device_id=target[side],
            device_id_type=MESH,
        )

    def start(pairs):
        for side, copy in pairs:

            @pl.when(has[side])
            def _(copy=copy):
                copy.start()

    def start_ordered(pairs):
        gx_odd = gx % 2 == 1

        @pl.when(gx_odd)
        def _():
            start([pair for pair in pairs if pair[0] == "xh"])
            start([pair for pair in pairs if pair[0] == "xl"])

        @pl.when(jnp.logical_not(gx_odd))
        def _():
            start([pair for pair in pairs if pair[0] == "xl"])
            start([pair for pair in pairs if pair[0] == "xh"])

    def wait_sent(pairs):
        for side, copy in pairs:

            @pl.when(has[side])
            def _(copy=copy):
                copy.wait_send()

    def wait_got(pairs):
        for side, copy in pairs:

            @pl.when(has[opposite[side]])
            def _(copy=copy):
                copy.wait_recv()

    def zero(ref):
        ref[...] = jnp.zeros(ref.shape, ref.dtype)

    def zero_unless(side, *refs):
        @pl.when(jnp.logical_not(has[side]))
        def _():
            for ref in refs:
                zero(ref)

    @pl.when(even)
    def _():
        pl.semaphore_wait(barrier, 1 + one_if(has["zl"]))
        signal(pair_sem, (gx, gz + 1))

        @pl.when(has["zl"])
        def _():
            signal(pair_sem, (gx, gz - 1))

    @pl.when(odd)
    def _():
        pl.semaphore_wait(pair_sem, 1 + one_if(has["zh"]))

    pz_copies = [
        ("zh", described("zh", plas_in, PZH.at[0], 0, 0)),
        ("zl", described("zl", plas_in, PZH.at[1], 0, 0)),
    ]
    start(pz_copies)
    vel_load.start()
    for copy in rest_loads:
        copy.start()
    weak_load.start()

    places_a = lax.broadcasted_iota(jnp.int32, (ny, ny), 0)
    places_b = lax.broadcasted_iota(jnp.int32, (ny, ny), 1)
    gap = (places_a - places_b).astype(jnp.float32)
    YM[...] = jnp.where(
        jnp.abs(gap) <= float(REACH), jnp.exp(-gap * gap / 18.0) / weight_total, 0.0
    )
    zero_unless("zl", PZH.at[0])
    zero_unless("zh", PZH.at[1])
    zero_unless("xl", V.at[:, pl.ds(0, 1)], GXH.at[0], XH.at[0], XHL.at[0], RF.at[:, pl.ds(0, 1)])
    zero_unless("xh", V.at[:, pl.ds(rows + 1, 1)], GXH.at[1], XH.at[1], XHL.at[1])
    zero_unless("xh", RF.at[:, pl.ds(rows + 1, 1)])
    zero_unless("zl", VZH.at[0], ZH.at[0], ZHL.at[0], RZF.at[0])
    zero_unless("zh", VZH.at[1], ZH.at[1], ZHL.at[1], RZF.at[1])
    for number, (a, b) in enumerate(corners):
        zero_unless(a + b, CH.at[number])
    for it in range(ITERS):
        zero(SX.at[it, :, pl.ds(0, 1)])
        zero(SX.at[it, :, pl.ds(rows + 1, 1)])

    @pl.when(odd)
    def _():
        greeters = 2 * (one_if(has["xl"]) + one_if(has["xh"]))
        for _, _, there in met:
            greeters = greeters + one_if(there)
        pl.semaphore_wait(barrier, greeters)
        signal(pair_sem, (gx, gz - 1))

    @pl.when(even)
    def _():
        pl.semaphore_wait(pair_sem, 1)

    vel_copies = [
        ("xh", described("xh", vel_in.at[:, pl.ds(rows - 1, 1)], V.at[:, pl.ds(0, 1)], 2, 2)),
        ("xl", described("xl", vel_in.at[:, pl.ds(0, 1)], V.at[:, pl.ds(rows + 1, 1)], 2, 2)),
    ]
    start_ordered(vel_copies)

    def hop_send(k):
        if k < len(rounds):

            @pl.when(odd)
            def _():
                for x_place, z_place, there in rounds[k]:

                    @pl.when(there)
                    def _(x_place=x_place, z_place=z_place):
                        signal(hop_sem.at[k], (x_place, z_place))

    def hop_wait(k):
        if k < len(rounds):

            @pl.when(odd)
            def _():
                expected = 0
                for _, _, there in rounds[k]:
                    expected = expected + one_if(there)
                pl.semaphore_wait(hop_sem.at[k], expected)

    hop_send(0)

    block = next(size for size in (BLOCK, 4, 2, 1) if rows % size == 0)
    many = (block, nz, ny)

    def over_rows(body, carry=0):
        return lax.fori_loop(0, rows // block, lambda i, state: body(i * block, state), carry)

    def at(x):
        return pl.ds(x, block)

    vel_load.wait()

    def vel_edges(x, carry):
        for c in range(3):
            row = V[c, at(x + 1)]
            VZE[0, c, at(x)] = row[:, 0:1]
            VZE[1, c, at(x)] = row[:, nz - 1 : nz]
        return carry

    over_rows(vel_edges)
    plas_load.wait()
    wait_got(pz_copies)
    vz_copies = [
        ("zh", described("zh", VZE.at[1], VZH.at[0], 1, 1)),
        ("zl", described("zl", VZE.at[0], VZH.at[1], 1, 1)),
    ]
    start(vz_copies)

    def smooth_z(x, carry):
        own, low, high = PLZ[at(x)], PZH[0, at(x)], PZH[1, at(x)]
        sub = lax.broadcasted_iota(jnp.int32, many, 1)
        sum_ = gauss_weights[REACH] * own
        for k in range(1, REACH + 1):
            above = pltpu.roll(jnp.where(sub >= k, own, high), nz - k, 1)
            below = pltpu.roll(jnp.where(sub < nz - k, own, low), k, 1)
            sum_ = sum_ + gauss_weights[REACH + k] * (above + below)
        SM[at(x)] = sum_
        return carry

    over_rows(smooth_z)
    GX[...] = jnp.dot(
        SM[...].reshape(rows * nz, ny),
        YM[...],
        precision=lax.Precision.HIGHEST,
        preferred_element_type=jnp.float32,
    ).reshape(rows, nz, ny)
    plas_copies = [
        ("xh", described("xh", GX.at[pl.ds(rows - REACH, REACH)], GXH.at[0], 3, 3)),
        ("xl", described("xl", GX.at[pl.ds(0, REACH)], GXH.at[1], 3, 3)),
    ]
    start_ordered(plas_copies)
    hop_wait(0)
    hop_send(1)

    all_rest.wait()
    weak_load.wait()

    def prepare(x, carry):
        eta = VI[at(x)]
        eta = shear_time_increment * eta / (eta + shear_time_increment)
        ETA[at(x)] = eta
        INV[at(x)] = 1.0 / (eta + 0.5)
        COH[at(x)] = 0.8660254 - (0.8660254 * 0.6) * WK[at(x)].astype(jnp.float32)
        return carry

    over_rows(prepare)
    for row in range(rows):
        sum_ = gauss_weights[REACH] * GX[row]
        for k in range(1, REACH + 1):
            for other in (row - k, row + k):
                if 0 <= other < rows:
                    sum_ = sum_ + gauss_weights[REACH + k] * GX[other]
        SM[row] = sum_
    for k in range(1, len(rounds) - 1):
        hop_wait(k)
        hop_send(k + 1)

    wait_got(vz_copies)
    wait_got(vel_copies)

    def dy(f):
        lane = lax.broadcasted_iota(jnp.int32, f.shape, 2)
        up = jnp.where(lane < ny - 1, pltpu.roll(f, ny - 1, 2), 0.0)
        down = jnp.where(lane > 0, pltpu.roll(f, 1, 2), 0.0)
        return (up - down) * 0.5

    def dz(f, low, high):
        sub = lax.broadcasted_iota(jnp.int32, f.shape, 1)
        up = pltpu.roll(jnp.where(sub >= 1, f, jnp.broadcast_to(high, f.shape)), nz - 1, 1)
        down = pltpu.roll(jnp.where(sub < nz - 1, f, jnp.broadcast_to(low, f.shape)), 1, 1)
        return (up - down) * 0.5

    def dz_inside(f):
        sub = lax.broadcasted_iota(jnp.int32, f.shape, 1)
        up = jnp.where(sub < nz - 1, pltpu.roll(f, nz - 1, 1), 0.0)
        down = jnp.where(sub >= 1, pltpu.roll(f, 1, 1), 0.0)
        return (up - down) * 0.5

    def strains(field, halo, x, size):
        v = [field[c, pl.ds(x + 1, size)] for c in range(3)]
        dx_v = [(field[c, pl.ds(x + 2, size)] - field[c, pl.ds(x, size)]) * 0.5 for c in range(3)]
        dz_v = [dz(f, halo[0, c, pl.ds(x, size)], halo[1, c, pl.ds(x, size)]) for c, f in enumerate(v)]
        dy_v = [dy(f) for f in v]
        div = dx_v[0] + dz_v[1] + dy_v[2]
        third = div * (1.0 / 3.0)
        return (
            dx_v[0] - third,
            dz_v[1] - third,
            dy_v[2] - third,
            0.5 * (dx_v[1] + dz_v[0]),
            0.5 * (dx_v[2] + dy_v[0]),
            0.5 * (dz_v[2] + dy_v[1]),
        ), div

    def second_invariant(trial):
        return jnp.sqrt(
            0.5 * (trial[0] * trial[0] + trial[1] * trial[1] + trial[2] * trial[2])
            + trial[3] * trial[3]
            + trial[4] * trial[4]
            + trial[5] * trial[5]
        )

    def first_trial(x, carry):
        strain, div = strains(V, VZH, x, block)
        quarter = 0.25 * div
        pres = PIN[at(x)] - quarter
        PR[at(x)] = pres
        PIN[at(x)] = pres - quarter
        twice = 2.0 * ETA[at(x)]
        trial = [
            twice * (strain[c] + IN[2 + c, at(x)] * (0.5 / shear_time_increment)) for c in range(6)
        ]
        for c in range(6):
            TAU[c, at(x)] = trial[c]
        TB[at(x)] = second_invariant(trial)
        return carry

    over_rows(first_trial)
    if len(rounds) > 1:
        hop_wait(len(rounds) - 1)

    @pl.when(odd)
    def _():
        signal(pair_sem, (gx, gz - 1))

    wait_got(plas_copies)
    for row in range(min(REACH, rows)):
        low, high = SM[row], SM[rows - 1 - row]
        for k in range(row + 1, REACH + 1):
            low = low + gauss_weights[REACH + k] * GXH[0, REACH + row - k]
            high = high + gauss_weights[REACH + k] * GXH[1, k - 1 - row]
        SM[row] = low
        SM[rows - 1 - row] = high

    half = ny // 2 if ny % 256 == 0 else ny

    def stress_rows(it, x, carry, pres, trial, tau_ii, strength, plas, edge):
        last = it == ITERS - 1
        most_f, most_eta = carry
        eta, inv = ETA[at(x)], INV[at(x)]
        yield_f = tau_ii - 0.5 * jnp.maximum(pres, 0.0) - strength
        dlam = jnp.maximum(yield_f, 0.0) * inv
        shrink = 1.0 - eta * dlam / jnp.maximum(tau_ii, 0.5)
        tau = [shrink * value for value in trial]
        PL[at(x)] = plas + dlam
        if last:
            for c in range(6):
                TAU[c, at(x)] = tau[c]
        SX[it, 0, at(x + 1)] = tau[0] - pres
        SX[it, 1, at(x + 1)] = tau[3]
        SX[it, 2, at(x + 1)] = tau[4]
        szz = tau[1] - pres
        TZ[0, at(x)] = szz
        TZ[1, at(x)] = tau[5]
        TZ[2, at(x)] = tau[2] - pres
        for c, f in enumerate((tau[3], szz, tau[5])):
            edge[0, c, at(x)] = f[:, 0:1]
            edge[1, c, at(x)] = f[:, nz - 1 : nz]
        return jnp.maximum(most_f, yield_f), jnp.maximum(most_eta, eta * shrink)

    def forces(it, x, size, diff_z):
        s = [SX[it, c, pl.ds(x + 1, size)] for c in range(3)]
        t = [TZ[c, pl.ds(x, size)] for c in range(3)]
        along_x = [0.5 * (SX[it, c, pl.ds(x + 2, size)] - SX[it, c, pl.ds(x, size)]) for c in range(3)]
        along_z = [diff_z(c, f) for c, f in enumerate((s[1], t[0], t[1]))]
        along_y = [dy(f) for f in (s[2], t[1], t[2])]
        return [along_x[c] + along_z[c] + along_y[c] for c in range(3)]

    def folded(most):
        most = jnp.max(jnp.max(most, axis=0), axis=0, keepdims=True)
        return jnp.maximum(most[:, :half], most[:, ny - half :])

    def tell(it, place):
        pltpu.make_async_remote_copy(
            src_ref=PK.at[it, me],
            dst_ref=PK.at[it, me],
            send_sem=pk_send,
            recv_sem=pk_recv.at[it],
            device_id=place,
            device_id_type=MESH,
        ).start()

    def tell_all(it, most_f, most_eta):
        PK[it, me] = jnp.concatenate([folded(most_f), folded(most_eta)], axis=0)
        for dz_ in range(gz_count):
            other_z = gz + dz_
            other_z = jnp.where(other_z >= gz_count, other_z - gz_count, other_z)

            def one(dx_, carry, other_z=other_z):
                other_x = gx + dx_
                tell(it, (jnp.where(other_x >= gx_count, other_x - gx_count, other_x), other_z))
                return carry

            first = 0 if dz_ else 1
            if gx_count <= 16 and gz_count <= 2:
                for dx_ in range(first, gx_count):
                    one(dx_, 0)
            else:
                lax.fori_loop(first, gx_count, one, 0)

    def told(it):
        others = PK.at[it, pl.ds(0, total - 1)]
        pltpu.make_async_copy(others, others, pk_recv.at[it]).wait()
        peaks = jnp.max(PK[it], axis=0)
        step = 0.125 / jnp.max(peaks[1:2], axis=1, keepdims=True)
        return step, jnp.max(peaks[0:1], axis=1, keepdims=True)

    def tell_sent():
        others = PK.at[0, pl.ds(0, total - 1)]
        pltpu.make_async_copy(others, others, pk_send).wait()

    lowest = jnp.full(many, -jnp.inf, jnp.float32)

    def first_stress(x, carry):
        strength = COH[at(x)] / (1.0 + 2.0 * SM[at(x)])
        COH[at(x)] = strength
        trial = [TAU[c, at(x)] for c in range(6)]
        return stress_rows(0, x, carry, PR[at(x)], trial, TB[at(x)], strength, PLZ[at(x)], SE)

    most_f, most_eta = over_rows(first_stress, (lowest, lowest))

    @pl.when(even)
    def _():
        pl.semaphore_wait(pair_sem, 1)

    tell_all(0, most_f, most_eta)
    wait_sent(vel_copies)
    for number, row in ((0, 0), (1, rows - 1)):
        force = forces(0, row, 1, lambda c, f: dz_inside(f))
        for c in range(3):
            XS[number, c] = SX[0, c, row + 1]
            XS[number, 3 + c] = force[c][0]
        for layer in range(2):
            where = 2 * number + layer
            place = (nz - 1) * layer
            for c in range(3):
                CE[where, c] = SX[0, c, row + 1, place : place + 1]
                CE[where, 3 + c] = SE[layer, c, row]
    x_copies = [
        ("xh", described("xh", XS.at[1], XH.at[0], 4, 2)),
        ("xl", described("xl", XS.at[0], XH.at[1], 4, 2)),
    ]
    start_ordered(x_copies)
    corner_copies = []
    for number, (a, b) in enumerate(corners):
        there = corners.index((opposite[a], opposite[b]))
        corner_copies.append(
            (
                a + b,
                pltpu.make_async_remote_copy(
                    src_ref=CE.at[number],
                    dst_ref=CH.at[there],
                    send_sem=send_sem.at[8 + number],
                    recv_sem=recv_sem.at[10 + number],
                    device_id=target[a + b],
                    device_id_type=MESH,
                ),
            )
        )
    start(corner_copies)

    def own_force(x, carry):
        force = forces(0, x, block, lambda c, f: dz_inside(f))
        for c in range(3):
            RF[c, at(x + 1)] = force[c]
            SE[0, 3 + c, at(x)] = force[c][:, 0:1]
            SE[1, 3 + c, at(x)] = force[c][:, nz - 1 : nz]
        return carry

    over_rows(own_force)
    wait_sent(pz_copies)
    z_copies = [
        ("zh", described("zh", SE.at[1], ZH.at[0], 0, 0)),
        ("zl", described("zl", SE.at[0], ZH.at[1], 0, 0)),
    ]
    start(z_copies)
    wait_got(z_copies)

    def add_z(x, carry):
        sub = lax.broadcasted_iota(jnp.int32, many, 1)
        for c in range(3):
            high = jnp.where(sub == nz - 1, jnp.broadcast_to(ZH[1, c, at(x)], many), 0.0)
            low = jnp.where(sub == 0, jnp.broadcast_to(ZH[0, c, at(x)], many), 0.0)
            RF[c, at(x + 1)] = RF[c, at(x + 1)] + 0.5 * (high - low)
        return carry

    def second_trial(x, size):
        strain, div = strains(RF, RZF, x, size)
        twice = 2.0 * ETA[pl.ds(x, size)]
        for c in range(6):
            TR[c, pl.ds(x, size)] = twice * strain[c]
        DV[pl.ds(x, size)] = 0.25 * div

    over_rows(add_z)

    @pl.when(has["zl"])
    def _():
        RZF[0] = ZH[0, 3:6] + 0.5 * SE[0, 0:3]

    @pl.when(has["zh"])
    def _():
        RZF[1] = ZH[1, 3:6] - 0.5 * SE[1, 0:3]

    inside = rows - 4
    if inside > 0:
        size = next(size for size in (6, 4, 3, 2, 1) if inside % size == 0)

        def inside_trial(i, carry):
            second_trial(2 + i * size, size)
            return carry

        lax.fori_loop(0, inside // size, inside_trial, 0)

    wait_got(x_copies)
    wait_got(corner_copies)
    for number, side, row in ((0, "xl", 0), (1, "xh", rows - 1)):
        sign = 0.5 - number
        beyond = row + 2 * number
        for c in range(3):
            RF[c, row + 1] = RF[c, row + 1] - sign * XH[number, c]

        @pl.when(has[side])
        def _(number=number, sign=sign, row=row, beyond=beyond):
            sub = lax.broadcasted_iota(jnp.int32, (nz, ny), 0)
            for c in range(3):
                low = jnp.where(sub == 0, jnp.broadcast_to(CH[2 * number, 3 + c], (nz, ny)), 0.0)
                high = jnp.where(sub == nz - 1, jnp.broadcast_to(CH[2 * number + 1, 3 + c], (nz, ny)), 0.0)
                RF[c, beyond] = XH[number, 3 + c] + sign * SX[0, c, row + 1] + 0.5 * (high - low)

        for layer in range(2):
            for c in range(3):
                RZF[layer, c, row] = RZF[layer, c, row] - sign * CH[2 * number + layer, c]
    if inside > 0:
        second_trial(0, 2)
        second_trial(rows - 2, 2)
    else:
        second_trial(0, rows)

    step, top = told(0)
    tell_sent()
    tops = [top]

    def second_stress(x, carry):
        pres = PIN[at(x)] - step * DV[at(x)]
        PR[at(x)] = pres
        trial = [TAU[c, at(x)] + step * TR[c, at(x)] for c in range(6)]
        return stress_rows(
            1, x, carry, pres, trial, second_invariant(trial), COH[at(x)], PL[at(x)], SEL
        )

    most_f, most_eta = over_rows(second_stress, (lowest, lowest))
    tell_all(1, most_f, most_eta)
    wait_sent(plas_copies)
    wait_sent(vz_copies)
    sx_copies = [
        ("xh", described("xh", SX.at[1, :, pl.ds(rows, 1)], XHL.at[0], 2, 3)),
        ("xl", described("xl", SX.at[1, :, pl.ds(1, 1)], XHL.at[1], 2, 3)),
    ]
    start_ordered(sx_copies)
    sz_copies = [
        ("zh", described("zh", SEL.at[1], ZHL.at[0], 1, 1)),
        ("zl", described("zl", SEL.at[0], ZHL.at[1], 1, 1)),
    ]
    start(sz_copies)

    def moved(x, carry):
        for c in range(3):
            V[c, at(x + 1)] = V[c, at(x + 1)] + step * RF[c, at(x + 1)]
        return carry

    over_rows(moved)
    wait_got(sz_copies)

    def last_force(x, carry):
        def diff_z(c, f):
            return dz(f, ZHL[0, c, at(x)], ZHL[1, c, at(x)])

        force = forces(1, x, block, diff_z)
        for c in range(3):
            RF[c, at(x + 1)] = force[c]
        return carry

    over_rows(last_force)
    wait_got(sx_copies)
    for c in range(3):
        RF[c, 1] = RF[c, 1] - 0.5 * XHL[0, c, 0]
        RF[c, rows] = RF[c, rows] + 0.5 * XHL[1, c, 0]
    step, top = told(1)
    tops.append(top)

    def last_velocity(x, carry):
        for c in range(3):
            VOUT[c, at(x)] = V[c, at(x + 1)] + step * RF[c, at(x + 1)]
        return carry

    over_rows(last_velocity)
    peak_out[...] = jnp.concatenate(tops, axis=1)[0]
    wait_sent(x_copies + corner_copies + z_copies + sx_copies + sz_copies)
    tell_sent()


def store_kernel(*refs):
    held, out, sem = refs[:5], refs[5:10], refs[10]
    copies = [pltpu.make_async_copy(a, b, sem.at[i]) for i, (a, b) in enumerate(zip(held, out))]
    for copy in copies:
        copy.start()
    for copy in copies:
        copy.wait()


def solution(mesh):
    gx_count, gz_count = mesh.shape["gx"], mesh.shape["gz"]
    total = gx_count * gz_count

    def per_device(velocity, pressure, stress_old, plastic, viscosity, weak_seed):
        rows, nz, ny = pressure.shape
        cells = (rows, nz, ny)
        f32 = jnp.float32
        vm = lambda *shape: pltpu.VMEM(shape, f32)
        hops = len(bits_of(gx_count)) + len(bits_of(gz_count // 2))
        anywhere = pl.BlockSpec(memory_space=pl.ANY)
        shapes = (velocity.shape, pressure.shape, stress_old.shape, plastic.shape)
        held = pl.pallas_call(
            functools.partial(kernel, gx_count, gz_count),
            out_shape=tuple(vm(*shape) for shape in shapes + ((ITERS,),)),
            in_specs=[anywhere] * 6,
            out_specs=(pl.BlockSpec(memory_space=pltpu.VMEM),) * 5,
            scratch_shapes=[
                vm(3, rows + 2, nz, ny),
                vm(8, *cells),
                pltpu.VMEM(cells, jnp.int32),
                vm(*cells),
                vm(2, *cells),
                vm(*cells),
                vm(*cells),
                vm(*cells),
                vm(ny, ny),
                vm(*cells),
                vm(2, REACH, nz, ny),
                vm(*cells),
                vm(2, 3, rows, 1, ny),
                vm(2, 3, rows, 1, ny),
                vm(ITERS, 3, rows + 2, nz, ny),
                vm(3, *cells),
                vm(2, 6, rows, 1, ny),
                vm(2, 6, rows, 1, ny),
                vm(2, 6, nz, ny),
                vm(2, 6, nz, ny),
                vm(4, 6, 1, ny),
                vm(4, 6, 1, ny),
                vm(2, 3, rows, 1, ny),
                vm(2, 3, rows, 1, ny),
                vm(2, 3, 1, nz, ny),
                vm(3, rows + 2, nz, ny),
                vm(2, 3, rows, 1, ny),
                vm(6, *cells),
                vm(*cells),
                vm(*cells),
                vm(ITERS, total, 2, ny // 2 if ny % 256 == 0 else ny),
                pltpu.SemaphoreType.DMA((4,)),
                pltpu.SemaphoreType.DMA((12,)),
                pltpu.SemaphoreType.DMA((14,)),
                pltpu.SemaphoreType.DMA,
                pltpu.SemaphoreType.DMA((ITERS,)),
                pltpu.SemaphoreType.REGULAR,
                pltpu.SemaphoreType.REGULAR((hops,)),
            ],
            compiler_params=pltpu.CompilerParams(collective_id=0, has_side_effects=True),
        )(velocity, pressure, stress_old, plastic, viscosity, weak_seed)
        held = [pltpu.with_memory_space_constraint(array, pltpu.VMEM) for array in held]
        return pl.pallas_call(
            store_kernel,
            out_shape=tuple(jax.ShapeDtypeStruct(shape, f32) for shape in shapes)
            + (jax.ShapeDtypeStruct((ITERS,), f32),),
            in_specs=[anywhere] * 5,
            out_specs=(anywhere,) * 5,
            scratch_shapes=[pltpu.SemaphoreType.DMA((5,))],
        )(*held)

    in_specs = (
        P(None, "gx", "gz", None),
        P("gx", "gz", None),
        P(None, "gx", "gz", None),
        P("gx", "gz", None),
        P("gx", "gz", None),
        P("gx", "gz", None),
    )
    out_specs = (
        P(None, "gx", "gz", None),
        P("gx", "gz", None),
        P(None, "gx", "gz", None),
        P("gx", "gz", None),
        P(),
    )
    return jax.shard_map(
        per_device, mesh=mesh, in_specs=in_specs, out_specs=out_specs, check_vma=False
    )
```

time: 25.8 us -> 22.9 us (0.89)
  Pallas kernels: 25 us -> 22.1 us
    pallas_call x1, Pallas kernels: 23.9 us -> 20.9 us  [per_device(): pl.pallas_call(functools.partial(kernel, gx_count, gz_count), out_shape=t...]
where the time goes in v2:
time: 22.9 us; the launch traced here: 22.7 us
  Pallas kernels  22.1 us (97%)
  between operations  0.64 us (3%)
    pallas_call x1, Pallas kernels, per_device(): pl.pallas_call(functools.partial(kernel, gx_count, gz_count), out_shape=t...  20.9 us
    pallas_call x1, Pallas kernels, per_device(): pl.pallas_call(store_kernel, out_shape=tuple((jax.ShapeDtypeStruct(shape,...  1.14 us

profile of v2, /device:TPU:0, one launch (start us, length us, event | category | flops | bytes accessed | tf_op | source)
XLA Modules:
  0.0 22.7 jit_solution(8740527587235763066)
XLA Ops:
  0.6 20.9 %shard_map.101 = (f32[3,16,8,256]{3,2,1,0:T(8,128)S(1)}, f32[16,8,256]{2,1,0:T(8,128)S(1)}, f32[6,16,8,256]{3,2,1,0:T(8,128)S(1)}, f32[16,8,256]{2,1,0:T(8,128)S(1)}, f32[2]{0:T(128)S(1)}) custom-call(f32[3,16,8,256]{3,2,1,0:T(8,128)} %vel_in.1, f32[16,8,256]{2,1,0:T(8,128)} %pres_in.1, f32[6,16,8,256]{3,2,1,0:T(8,128)} %old_in.1, f32[16,8,256]{2,1,0:T(8,128)} %plas_in.1, ...), custom_call_target="tpu_custom_call" | custom-call | tf_op jit(solution)/shard_map/pallas_call | solution.py:745
  21.6 1.1 %shard_map.102 = (f32[3,16,8,256]{3,2,1,0:T(8,128)}, f32[16,8,256]{2,1,0:T(8,128)}, f32[6,16,8,256]{3,2,1,0:T(8,128)}, f32[16,8,256]{2,1,0:T(8,128)}, f32[2]{0:T(128)}) custom-call(f32[3,16,8,256]{3,2,1,0:T(8,128)S(1)} %get-tuple-element.10.refs_0_, f32[16,8,256]{2,1,0:T(8,128)S(1)} %get-tuple-element.11.refs_1_, ...), custom_call_target="tpu_custom_call" | custom-call | tf_op jit(solution)/shard_map/pallas_call | solution.py:793

commit v3 on v2

--- a/solution.py
+++ b/solution.py
@@ -10,7 +10,6 @@
 
 ITERS = 2
 REACH = 6
-BLOCK = 8
 PLANE = 4
 MESH = pl.DeviceIdType.MESH
 
@@ -69,6 +68,7 @@
     TR,
     DV,
     TB,
+    MOST,
     PK,
     in_sem,
     send_sem,
@@ -182,18 +182,26 @@
             def _(copy=copy):
                 copy.start()
 
-    def start_ordered(pairs):
-        gx_odd = gx % 2 == 1
-
-        @pl.when(gx_odd)
-        def _():
-            start([pair for pair in pairs if pair[0] == "xh"])
-            start([pair for pair in pairs if pair[0] == "xl"])
-
-        @pl.when(jnp.logical_not(gx_odd))
-        def _():
-            start([pair for pair in pairs if pair[0] == "xl"])
-            start([pair for pair in pairs if pair[0] == "xh"])
+    gx_odd = gx % 2 == 1
+    gx_even = gx % 2 == 0
+
+    def start_far(pairs):
+        for place, side in ((gx_odd, "xh"), (gx_even, "xl")):
+
+            @pl.when(place)
+            def _(side=side):
+                start([pair for pair in pairs if pair[0] == side])
+
+    def start_near(pairs):
+        for place, side in ((gx_odd, "xl"), (gx_even, "xh")):
+
+            @pl.when(place)
+            def _(side=side):
+                start([pair for pair in pairs if pair[0] == side])
+
+    has_far = jnp.logical_or(
+        jnp.logical_and(gx_odd, has["xh"]), jnp.logical_and(gx_even, has["xl"])
+    )
 
     def wait_sent(pairs):
         for side, copy in pairs:
@@ -276,7 +284,12 @@
         ("xh", described("xh", vel_in.at[:, pl.ds(rows - 1, 1)], V.at[:, pl.ds(0, 1)], 2, 2)),
         ("xl", described("xl", vel_in.at[:, pl.ds(0, 1)], V.at[:, pl.ds(rows + 1, 1)], 2, 2)),
     ]
-    start_ordered(vel_copies)
+    start_far(vel_copies)
+
+    @pl.when(jnp.logical_not(has_far))
+    def _():
+        start_near(vel_copies)
+
 
     def hop_send(k):
         if k < len(rounds):
@@ -301,7 +314,7 @@
 
     hop_send(0)
 
-    block = next(size for size in (BLOCK, 4, 2, 1) if rows % size == 0)
+    block = rows // 2
     many = (block, nz, ny)
 
     def over_rows(body, carry=0):
@@ -350,7 +363,13 @@
         ("xh", described("xh", GX.at[pl.ds(rows - REACH, REACH)], GXH.at[0], 3, 3)),
         ("xl", described("xl", GX.at[pl.ds(0, REACH)], GXH.at[1], 3, 3)),
     ]
-    start_ordered(plas_copies)
+    start_far(plas_copies)
+
+    @pl.when(has_far)
+    def _():
+        start_near(vel_copies)
+
+    start_near(plas_copies)
     hop_wait(0)
     hop_send(1)
 
@@ -378,7 +397,6 @@
         hop_send(k + 1)
 
     wait_got(vz_copies)
-    wait_got(vel_copies)
 
     def dy(f):
         lane = lax.broadcasted_iota(jnp.int32, f.shape, 2)
@@ -422,7 +440,7 @@
             + trial[5] * trial[5]
         )
 
-    def first_trial(x, carry):
+    def first_trial(x):
         strain, div = strains(V, VZH, x, block)
         quarter = 0.25 * div
         pres = PIN[at(x)] - quarter
@@ -435,9 +453,20 @@
         for c in range(6):
             TAU[c, at(x)] = trial[c]
         TB[at(x)] = second_invariant(trial)
-        return carry
-
-    over_rows(first_trial)
+
+    def in_order(act):
+        for place, numbers in ((gx_odd, (1, 0)), (gx_even, (0, 1))):
+
+            @pl.when(place)
+            def _(numbers=numbers):
+                for number in numbers:
+                    act(number, number == numbers[0])
+
+    def one_trial(number, far):
+        wait_got(vel_copies[number : number + 1])
+        first_trial(number * block)
+
+    in_order(one_trial)
     if len(rounds) > 1:
         hop_wait(len(rounds) - 1)
 
@@ -445,20 +474,10 @@
     def _():
         signal(pair_sem, (gx, gz - 1))
 
-    wait_got(plas_copies)
-    for row in range(min(REACH, rows)):
-        low, high = SM[row], SM[rows - 1 - row]
-        for k in range(row + 1, REACH + 1):
-            low = low + gauss_weights[REACH + k] * GXH[0, REACH + row - k]
-            high = high + gauss_weights[REACH + k] * GXH[1, k - 1 - row]
-        SM[row] = low
-        SM[rows - 1 - row] = high
-
     half = ny // 2 if ny % 256 == 0 else ny
 
-    def stress_rows(it, x, carry, pres, trial, tau_ii, strength, plas, edge):
+    def stress_rows(it, x, pres, trial, tau_ii, strength, plas, edge):
         last = it == ITERS - 1
-        most_f, most_eta = carry
         eta, inv = ETA[at(x)], INV[at(x)]
         yield_f = tau_ii - 0.5 * jnp.maximum(pres, 0.0) - strength
         dlam = jnp.maximum(yield_f, 0.0) * inv
@@ -478,7 +497,7 @@
         for c, f in enumerate((tau[3], szz, tau[5])):
             edge[0, c, at(x)] = f[:, 0:1]
             edge[1, c, at(x)] = f[:, nz - 1 : nz]
-        return jnp.maximum(most_f, yield_f), jnp.maximum(most_eta, eta * shrink)
+        return yield_f, eta * shrink
 
     def forces(it, x, size, diff_z):
         s = [SX[it, c, pl.ds(x + 1, size)] for c in range(3)]
@@ -502,8 +521,9 @@
             device_id_type=MESH,
         ).start()
 
-    def tell_all(it, most_f, most_eta):
-        PK[it, me] = jnp.concatenate([folded(most_f), folded(most_eta)], axis=0)
+    def tell_all(it):
+        most = [folded(jnp.maximum(MOST[0, k], MOST[1, k])) for k in range(2)]
+        PK[it, me] = jnp.concatenate(most, axis=0)
         for dz_ in range(gz_count):
             other_z = gz + dz_
             other_z = jnp.where(other_z >= gz_count, other_z - gz_count, other_z)
@@ -531,38 +551,16 @@
         others = PK.at[0, pl.ds(0, total - 1)]
         pltpu.make_async_copy(others, others, pk_send).wait()
 
-    lowest = jnp.full(many, -jnp.inf, jnp.float32)
-
-    def first_stress(x, carry):
+    def first_stress(x):
         strength = COH[at(x)] / (1.0 + 2.0 * SM[at(x)])
         COH[at(x)] = strength
         trial = [TAU[c, at(x)] for c in range(6)]
-        return stress_rows(0, x, carry, PR[at(x)], trial, TB[at(x)], strength, PLZ[at(x)], SE)
-
-    most_f, most_eta = over_rows(first_stress, (lowest, lowest))
-
-    @pl.when(even)
-    def _():
-        pl.semaphore_wait(pair_sem, 1)
-
-    tell_all(0, most_f, most_eta)
-    wait_sent(vel_copies)
-    for number, row in ((0, 0), (1, rows - 1)):
-        force = forces(0, row, 1, lambda c, f: dz_inside(f))
-        for c in range(3):
-            XS[number, c] = SX[0, c, row + 1]
-            XS[number, 3 + c] = force[c][0]
-        for layer in range(2):
-            where = 2 * number + layer
-            place = (nz - 1) * layer
-            for c in range(3):
-                CE[where, c] = SX[0, c, row + 1, place : place + 1]
-                CE[where, 3 + c] = SE[layer, c, row]
+        return stress_rows(0, x, PR[at(x)], trial, TB[at(x)], strength, PLZ[at(x)], SE)
+
     x_copies = [
         ("xh", described("xh", XS.at[1], XH.at[0], 4, 2)),
         ("xl", described("xl", XS.at[0], XH.at[1], 4, 2)),
     ]
-    start_ordered(x_copies)
     corner_copies = []
     for number, (a, b) in enumerate(corners):
         there = corners.index((opposite[a], opposite[b]))
@@ -579,6 +577,39 @@
                 ),
             )
         )
+
+    def one_side(number, far):
+        row = (rows - 1) * number
+        wait_got(plas_copies[number : number + 1])
+        for beside in range(min(REACH, block)):
+            here = beside if number == 0 else rows - 1 - beside
+            sum_ = SM[here]
+            for k in range(beside + 1, REACH + 1):
+                place = REACH + beside - k if number == 0 else k - 1 - beside
+                sum_ = sum_ + gauss_weights[REACH + k] * GXH[number, place]
+            SM[here] = sum_
+        MOST[number, 0], MOST[number, 1] = first_stress(number * block)
+        force = forces(0, row, 1, lambda c, f: dz_inside(f))
+        for c in range(3):
+            XS[number, c] = SX[0, c, row + 1]
+            XS[number, 3 + c] = force[c][0]
+        for layer in range(2):
+            where = 2 * number + layer
+            place = (nz - 1) * layer
+            for c in range(3):
+                CE[where, c] = SX[0, c, row + 1, place : place + 1]
+                CE[where, 3 + c] = SE[layer, c, row]
+        if far:
+            wait_sent(vel_copies)
+            start(x_copies[1 - number : 2 - number])
+
+    in_order(one_side)
+    @pl.when(even)
+    def _():
+        pl.semaphore_wait(pair_sem, 1)
+
+    tell_all(0)
+    start_near(x_copies)
     start(corner_copies)
 
     def own_force(x, carry):
@@ -662,23 +693,26 @@
     tell_sent()
     tops = [top]
 
-    def second_stress(x, carry):
+    def second_stress(i, carry):
+        x = i * block
         pres = PIN[at(x)] - step * DV[at(x)]
         PR[at(x)] = pres
         trial = [TAU[c, at(x)] + step * TR[c, at(x)] for c in range(6)]
-        return stress_rows(
-            1, x, carry, pres, trial, second_invariant(trial), COH[at(x)], PL[at(x)], SEL
+        MOST[i, 0], MOST[i, 1] = stress_rows(
+            1, x, pres, trial, second_invariant(trial), COH[at(x)], PL[at(x)], SEL
         )
-
-    most_f, most_eta = over_rows(second_stress, (lowest, lowest))
-    tell_all(1, most_f, most_eta)
+        return carry
+
+    lax.fori_loop(0, 2, second_stress, 0)
+    tell_all(1)
     wait_sent(plas_copies)
     wait_sent(vz_copies)
     sx_copies = [
         ("xh", described("xh", SX.at[1, :, pl.ds(rows, 1)], XHL.at[0], 2, 3)),
         ("xl", described("xl", SX.at[1, :, pl.ds(1, 1)], XHL.at[1], 2, 3)),
     ]
-    start_ordered(sx_copies)
+    start_far(sx_copies)
+    start_near(sx_copies)
     sz_copies = [
         ("zh", described("zh", SEL.at[1], ZHL.at[0], 1, 1)),
         ("zl", described("zl", SEL.at[0], ZHL.at[1], 1, 1)),
@@ -778,6 +812,7 @@
                 vm(6, *cells),
                 vm(*cells),
                 vm(*cells),
+                vm(2, 2, rows // 2, nz, ny),
                 vm(ITERS, total, 2, ny // 2 if ny % 256 == 0 else ny),
                 pltpu.SemaphoreType.DMA((4,)),
                 pltpu.SemaphoreType.DMA((12,)),

time: 22.9 us -> 22.2 us (0.969)
  Pallas kernels: 22.1 us -> 21.4 us
    pallas_call x1, Pallas kernels: 20.9 us -> 20.3 us  [per_device(): pl.pallas_call(functools.partial(kernel, gx_count, gz_count), out_shape=t...]
where the time goes in v3:
time: 22.2 us; the launch traced here: 22.1 us
  Pallas kernels  21.4 us (96%)
  between operations  0.64 us (3%)
    pallas_call x1, Pallas kernels, per_device(): pl.pallas_call(functools.partial(kernel, gx_count, gz_count), out_shape=t...  20.3 us
    pallas_call x1, Pallas kernels, per_device(): pl.pallas_call(store_kernel, out_shape=tuple((jax.ShapeDtypeStruct(shape,...  1.14 us

profile of v3, /device:TPU:0, one launch (start us, length us, event | category | flops | bytes accessed | tf_op | source)
XLA Modules:
  0.0 22.1 jit_solution(14109373168825698020)
XLA Ops:
  0.6 20.3 %shard_map.101 = (f32[3,16,8,256]{3,2,1,0:T(8,128)S(1)}, f32[16,8,256]{2,1,0:T(8,128)S(1)}, f32[6,16,8,256]{3,2,1,0:T(8,128)S(1)}, f32[16,8,256]{2,1,0:T(8,128)S(1)}, f32[2]{0:T(128)S(1)}) custom-call(f32[3,16,8,256]{3,2,1,0:T(8,128)} %vel_in.1, f32[16,8,256]{2,1,0:T(8,128)} %pres_in.1, f32[6,16,8,256]{3,2,1,0:T(8,128)} %old_in.1, f32[16,8,256]{2,1,0:T(8,128)} %plas_in.1, ...), custom_call_target="tpu_custom_call" | custom-call | tf_op jit(solution)/shard_map/pallas_call | solution.py:779
  20.9 1.1 %shard_map.102 = (f32[3,16,8,256]{3,2,1,0:T(8,128)}, f32[16,8,256]{2,1,0:T(8,128)}, f32[6,16,8,256]{3,2,1,0:T(8,128)}, f32[16,8,256]{2,1,0:T(8,128)}, f32[2]{0:T(128)}) custom-call(f32[3,16,8,256]{3,2,1,0:T(8,128)S(1)} %get-tuple-element.10.refs_0_, f32[16,8,256]{2,1,0:T(8,128)S(1)} %get-tuple-element.11.refs_1_, ...), custom_call_target="tpu_custom_call" | custom-call | tf_op jit(solution)/shard_map/pallas_call | solution.py:828

commit v4 on v3

--- a/solution.py
+++ b/solution.py
@@ -130,15 +130,15 @@
         return jnp.where(flag, 1, 0)
 
     VI, PIN = IN.at[0], IN.at[1]
-    plas_load = pltpu.make_async_copy(plas_in, PLZ, in_sem.at[0])
-    vel_load = pltpu.make_async_copy(vel_in, V.at[:, pl.ds(1, rows)], in_sem.at[1])
-    weak_load = pltpu.make_async_copy(weak_in, WK, in_sem.at[2])
+    plas_load = pltpu.make_async_copy(plas_in, PLZ, send_sem.at[6])
+    vel_load = pltpu.make_async_copy(vel_in, V.at[:, pl.ds(1, rows)], send_sem.at[2])
+    weak_load = pltpu.make_async_copy(weak_in, WK, pk_send)
     rest_loads = [
-        pltpu.make_async_copy(visc_in, VI, in_sem.at[3]),
-        pltpu.make_async_copy(pres_in, PIN, in_sem.at[3]),
-        pltpu.make_async_copy(old_in, IN.at[pl.ds(2, 6)], in_sem.at[3]),
-    ]
-    all_rest = pltpu.make_async_copy(IN, IN, in_sem.at[3])
+        pltpu.make_async_copy(visc_in, VI, in_sem),
+        pltpu.make_async_copy(pres_in, PIN, in_sem),
+        pltpu.make_async_copy(old_in, IN.at[pl.ds(2, 6)], in_sem),
+    ]
+    all_rest = pltpu.make_async_copy(IN, IN, in_sem)
 
     @pl.when(odd)
     def _():
@@ -467,16 +467,12 @@
         first_trial(number * block)
 
     in_order(one_trial)
-    if len(rounds) > 1:
-        hop_wait(len(rounds) - 1)
-
-    @pl.when(odd)
-    def _():
-        signal(pair_sem, (gx, gz - 1))
-
     half = ny // 2 if ny % 256 == 0 else ny
 
-    def stress_rows(it, x, pres, trial, tau_ii, strength, plas, edge):
+    def stress_rows(it, x, size, pres, trial, tau_ii, strength, plas, edge):
+        def at(x):
+            return pl.ds(x, size)
+
         last = it == ITERS - 1
         eta, inv = ETA[at(x)], INV[at(x)]
         yield_f = tau_ii - 0.5 * jnp.maximum(pres, 0.0) - strength
@@ -497,7 +493,7 @@
         for c, f in enumerate((tau[3], szz, tau[5])):
             edge[0, c, at(x)] = f[:, 0:1]
             edge[1, c, at(x)] = f[:, nz - 1 : nz]
-        return yield_f, eta * shrink
+        return jnp.max(yield_f, axis=0), jnp.max(eta * shrink, axis=0)
 
     def forces(it, x, size, diff_z):
         s = [SX[it, c, pl.ds(x + 1, size)] for c in range(3)]
@@ -508,7 +504,7 @@
         return [along_x[c] + along_z[c] + along_y[c] for c in range(3)]
 
     def folded(most):
-        most = jnp.max(jnp.max(most, axis=0), axis=0, keepdims=True)
+        most = jnp.max(most, axis=0, keepdims=True)
         return jnp.maximum(most[:, :half], most[:, ny - half :])
 
     def tell(it, place):
@@ -522,7 +518,8 @@
         ).start()
 
     def tell_all(it):
-        most = [folded(jnp.maximum(MOST[0, k], MOST[1, k])) for k in range(2)]
+        parts = 3 if it else 2
+        most = [folded(functools.reduce(jnp.maximum, [MOST[i, k] for i in range(parts)])) for k in range(2)]
         PK[it, me] = jnp.concatenate(most, axis=0)
         for dz_ in range(gz_count):
             other_z = gz + dz_
@@ -555,7 +552,7 @@
         strength = COH[at(x)] / (1.0 + 2.0 * SM[at(x)])
         COH[at(x)] = strength
         trial = [TAU[c, at(x)] for c in range(6)]
-        return stress_rows(0, x, PR[at(x)], trial, TB[at(x)], strength, PLZ[at(x)], SE)
+        return stress_rows(0, x, block, PR[at(x)], trial, TB[at(x)], strength, PLZ[at(x)], SE)
 
     x_copies = [
         ("xh", described("xh", XS.at[1], XH.at[0], 4, 2)),
@@ -570,7 +567,7 @@
                 pltpu.make_async_remote_copy(
                     src_ref=CE.at[number],
                     dst_ref=CH.at[there],
-                    send_sem=send_sem.at[8 + number],
+                    send_sem=send_sem.at[(2, 3, 6, 7)[number]],
                     recv_sem=recv_sem.at[10 + number],
                     device_id=target[a + b],
                     device_id_type=MESH,
@@ -602,6 +599,13 @@
         if far:
             wait_sent(vel_copies)
             start(x_copies[1 - number : 2 - number])
+        if far:
+            if len(rounds) > 1:
+                hop_wait(len(rounds) - 1)
+
+            @pl.when(odd)
+            def _():
+                signal(pair_sem, (gx, gz - 1))
 
     in_order(one_side)
     @pl.when(even)
@@ -610,6 +614,8 @@
 
     tell_all(0)
     start_near(x_copies)
+    wait_sent(vz_copies)
+    wait_sent(plas_copies)
     start(corner_copies)
 
     def own_force(x, carry):
@@ -663,6 +669,30 @@
             return carry
 
         lax.fori_loop(0, inside // size, inside_trial, 0)
+
+    step, top = told(0)
+    tell_sent()
+    tops = [top]
+
+    def second_stress(x, size):
+        here = pl.ds(x, size)
+        pres = PIN[here] - step * DV[here]
+        PR[here] = pres
+        trial = [TAU[c, here] + step * TR[c, here] for c in range(6)]
+        return stress_rows(
+            1, x, size, pres, trial, second_invariant(trial), COH[here], PL[here], SEL
+        )
+
+    lowest = jnp.full((nz, ny), -jnp.inf, jnp.float32)
+    most = (lowest, lowest)
+    if inside > 0:
+
+        def inside_stress(i, most):
+            f, eta = second_stress(2 + i * size, size)
+            return jnp.maximum(most[0], f), jnp.maximum(most[1], eta)
+
+        most = lax.fori_loop(0, inside // size, inside_stress, most)
+    MOST[2, 0], MOST[2, 1] = most
 
     wait_got(x_copies)
     wait_got(corner_copies)
@@ -689,30 +719,18 @@
     else:
         second_trial(0, rows)
 
-    step, top = told(0)
-    tell_sent()
-    tops = [top]
-
-    def second_stress(i, carry):
-        x = i * block
-        pres = PIN[at(x)] - step * DV[at(x)]
-        PR[at(x)] = pres
-        trial = [TAU[c, at(x)] + step * TR[c, at(x)] for c in range(6)]
-        MOST[i, 0], MOST[i, 1] = stress_rows(
-            1, x, pres, trial, second_invariant(trial), COH[at(x)], PL[at(x)], SEL
-        )
-        return carry
-
-    lax.fori_loop(0, 2, second_stress, 0)
+    for i, x in enumerate((0, rows - 2) if inside > 0 else (0,)):
+        MOST[i, 0], MOST[i, 1] = second_stress(x, 2 if inside > 0 else rows)
+    if inside <= 0:
+        MOST[1, 0], MOST[1, 1] = lowest, lowest
     tell_all(1)
-    wait_sent(plas_copies)
-    wait_sent(vz_copies)
+    wait_sent(corner_copies)
     sx_copies = [
         ("xh", described("xh", SX.at[1, :, pl.ds(rows, 1)], XHL.at[0], 2, 3)),
         ("xl", described("xl", SX.at[1, :, pl.ds(1, 1)], XHL.at[1], 2, 3)),
     ]
-    start_far(sx_copies)
-    start_near(sx_copies)
+    start(sx_copies[1:])
+    start(sx_copies[:1])
     sz_copies = [
         ("zh", described("zh", SEL.at[1], ZHL.at[0], 1, 1)),
         ("zl", described("zl", SEL.at[0], ZHL.at[1], 1, 1)),
@@ -751,7 +769,7 @@
 
     over_rows(last_velocity)
     peak_out[...] = jnp.concatenate(tops, axis=1)[0]
-    wait_sent(x_copies + corner_copies + z_copies + sx_copies + sz_copies)
+    wait_sent(x_copies + z_copies + sx_copies + sz_copies)
     tell_sent()
 
 
@@ -812,10 +830,10 @@
                 vm(6, *cells),
                 vm(*cells),
                 vm(*cells),
-                vm(2, 2, rows // 2, nz, ny),
+                vm(3, 2, nz, ny),
                 vm(ITERS, total, 2, ny // 2 if ny % 256 == 0 else ny),
-                pltpu.SemaphoreType.DMA((4,)),
-                pltpu.SemaphoreType.DMA((12,)),
+                pltpu.SemaphoreType.DMA,
+                pltpu.SemaphoreType.DMA((8,)),
                 pltpu.SemaphoreType.DMA((14,)),
                 pltpu.SemaphoreType.DMA,
                 pltpu.SemaphoreType.DMA((ITERS,)),

time: 22.2 us -> 21.7 us (0.977)
  Pallas kernels: 21.4 us -> 20.9 us
    pallas_call x1, Pallas kernels: 20.3 us -> 19.8 us  [per_device(): pl.pallas_call(functools.partial(kernel, gx_count, gz_count), out_shape=t...]
where the time goes in v4:
time: 21.7 us; the launch traced here: 21.6 us
  Pallas kernels  20.9 us (96%)
  between operations  0.64 us (3%)
    pallas_call x1, Pallas kernels, per_device(): pl.pallas_call(functools.partial(kernel, gx_count, gz_count), out_shape=t...  19.8 us
    pallas_call x1, Pallas kernels, per_device(): pl.pallas_call(store_kernel, out_shape=tuple((jax.ShapeDtypeStruct(shape,...  1.14 us

profile of v4, /device:TPU:0, one launch (start us, length us, event | category | flops | bytes accessed | tf_op | source)
XLA Modules:
  0.0 21.6 jit_solution(4910071101329238030)
XLA Ops:
  0.6 19.8 %shard_map.101 = (f32[3,16,8,256]{3,2,1,0:T(8,128)S(1)}, f32[16,8,256]{2,1,0:T(8,128)S(1)}, f32[6,16,8,256]{3,2,1,0:T(8,128)S(1)}, f32[16,8,256]{2,1,0:T(8,128)S(1)}, f32[2]{0:T(128)S(1)}) custom-call(f32[3,16,8,256]{3,2,1,0:T(8,128)} %vel_in.1, f32[16,8,256]{2,1,0:T(8,128)} %pres_in.1, f32[6,16,8,256]{3,2,1,0:T(8,128)} %old_in.1, f32[16,8,256]{2,1,0:T(8,128)} %plas_in.1, ...), custom_call_target="tpu_custom_call" | custom-call | tf_op jit(solution)/shard_map/pallas_call | solution.py:797
  20.4 1.1 %shard_map.102 = (f32[3,16,8,256]{3,2,1,0:T(8,128)}, f32[16,8,256]{2,1,0:T(8,128)}, f32[6,16,8,256]{3,2,1,0:T(8,128)}, f32[16,8,256]{2,1,0:T(8,128)}, f32[2]{0:T(128)}) custom-call(f32[3,16,8,256]{3,2,1,0:T(8,128)S(1)} %get-tuple-element.10.refs_0_, f32[16,8,256]{2,1,0:T(8,128)S(1)} %get-tuple-element.11.refs_1_, ...), custom_call_target="tpu_custom_call" | custom-call | tf_op jit(solution)/shard_map/pallas_call | solution.py:846

commit v5 on v4

--- a/solution.py
+++ b/solution.py
@@ -22,6 +22,24 @@
 def bits_of(count):
     assert count & (count - 1) == 0
     return [1 << bit for bit in range(count.bit_length() - 1)]
+
+
+def step_of(peaks):
+    lane = lax.broadcasted_iota(jnp.int32, peaks.shape, 1)
+    return 0.125 / jnp.max(jnp.where(lane < peaks.shape[1] // 2, -jnp.inf, peaks), axis=1, keepdims=True)
+
+
+def top_of(peaks):
+    lane = lax.broadcasted_iota(jnp.int32, peaks.shape, 1)
+    return jnp.max(jnp.where(lane < peaks.shape[1] // 2, peaks, -jnp.inf), axis=1, keepdims=True)
+
+
+def sides_of(count):
+    return min(count - 1, 2)
+
+
+def sems_of(z_sides):
+    return 2 * z_sides + 4, 2 * z_sides + 6 + 2 * z_sides
 
 
 def kernel(
@@ -33,11 +51,12 @@
     plas_in,
     visc_in,
     weak_in,
-    VOUT,
+    MOVED,
     PR,
     TAU,
     PL,
-    peak_out,
+    FORCE,
+    PEAKS,
     V,
     IN,
     WK,
@@ -129,9 +148,10 @@
     def one_if(flag):
         return jnp.where(flag, 1, 0)
 
+    z_sides = sides_of(gz_count)
     VI, PIN = IN.at[0], IN.at[1]
-    plas_load = pltpu.make_async_copy(plas_in, PLZ, send_sem.at[6])
-    vel_load = pltpu.make_async_copy(vel_in, V.at[:, pl.ds(1, rows)], send_sem.at[2])
+    plas_load = pltpu.make_async_copy(plas_in, PLZ, send_sem.at[sems_of(z_sides)[0] - 2])
+    vel_load = pltpu.make_async_copy(vel_in, V.at[:, pl.ds(1, rows)], send_sem.at[z_sides])
     weak_load = pltpu.make_async_copy(weak_in, WK, pk_send)
     rest_loads = [
         pltpu.make_async_copy(visc_in, VI, in_sem),
@@ -140,6 +160,12 @@
     ]
     all_rest = pltpu.make_async_copy(IN, IN, in_sem)
 
+    for side in ("xl", "xh"):
+
+        @pl.when(has[side])
+        def _(side=side):
+            signal(barrier, (target[side][0], lead))
+
     @pl.when(odd)
     def _():
         signal(barrier, (gx, gz - 1))
@@ -148,12 +174,6 @@
         def _():
             signal(barrier, (gx, gz + 1))
 
-    for side in ("xl", "xh"):
-
-        @pl.when(has[side])
-        def _(side=side):
-            signal(barrier, (target[side][0], lead))
-
     plas_load.start()
 
     @pl.when(odd)
@@ -164,13 +184,18 @@
             def _(x_place=x_place, z_place=z_place):
                 signal(barrier, (x_place, z_place))
 
+    def slot(group):
+        return group * z_sides if group < 2 else 2 * z_sides + 2 * (group - 2)
+
+    corner_sent = (slot(1), slot(1) + 1, slot(3), slot(3) + 1) if z_sides == 2 else (slot(1), slot(1), slot(3), slot(3))
+
     def described(side, source, landing, got, sent):
-        number = {"xl": 0, "xh": 1, "zl": 0, "zh": 1}.get(side, 0)
+        number = {"xl": 0, "xh": 1, "zl": 0, "zh": z_sides - 1}[side]
         return pltpu.make_async_remote_copy(
             src_ref=source,
             dst_ref=landing,
-            send_sem=send_sem.at[2 * sent + number],
-            recv_sem=recv_sem.at[2 * got + number],
+            send_sem=send_sem.at[slot(sent) + number],
+            recv_sem=recv_sem.at[slot(got) + number],
             device_id=target[side],
             device_id_type=MESH,
         )
@@ -504,7 +529,6 @@
         return [along_x[c] + along_z[c] + along_y[c] for c in range(3)]
 
     def folded(most):
-        most = jnp.max(most, axis=0, keepdims=True)
         return jnp.maximum(most[:, :half], most[:, ny - half :])
 
     def tell(it, place):
@@ -517,32 +541,42 @@
             device_id_type=MESH,
         ).start()
 
+    turned = {bit: flipped(gx, bit) - gx for bit in bits_of(gx_count)}
+
     def tell_all(it):
         parts = 3 if it else 2
-        most = [folded(functools.reduce(jnp.maximum, [MOST[i, k] for i in range(parts)])) for k in range(2)]
-        PK[it, me] = jnp.concatenate(most, axis=0)
-        for dz_ in range(gz_count):
-            other_z = gz + dz_
-            other_z = jnp.where(other_z >= gz_count, other_z - gz_count, other_z)
-
-            def one(dx_, carry, other_z=other_z):
-                other_x = gx + dx_
-                tell(it, (jnp.where(other_x >= gx_count, other_x - gx_count, other_x), other_z))
-                return carry
-
-            first = 0 if dz_ else 1
-            if gx_count <= 16 and gz_count <= 2:
-                for dx_ in range(first, gx_count):
-                    one(dx_, 0)
-            else:
-                lax.fori_loop(first, gx_count, one, 0)
+        most_f, most_eta = [
+            folded(functools.reduce(jnp.maximum, [MOST[i, k] for i in range(parts)])) for k in range(2)
+        ]
+        lane = lax.broadcasted_iota(jnp.int32, (nz, half), 1)
+        most_f = jnp.maximum(most_f, pltpu.roll(most_f, half // 2, 1))
+        most_eta = jnp.maximum(most_eta, pltpu.roll(most_eta, half // 2, 1))
+        PK[it, me] = jnp.max(jnp.where(lane < half // 2, most_f, most_eta), axis=0, keepdims=True)
+        if gx_count <= 16 and gz_count <= 2:
+            for flips in reversed(range(1, total)):
+                x_place, z_place = gx, gz
+                for bit in bits_of(gx_count):
+                    if flips // gz_count & bit:
+                        x_place = x_place + turned[bit]
+                if flips % gz_count:
+                    z_place = flipped(gz, 1)
+                tell(it, (x_place, z_place))
+        else:
+            for dz_ in range(gz_count):
+                other_z = gz + dz_
+                other_z = jnp.where(other_z >= gz_count, other_z - gz_count, other_z)
+
+                def one(dx_, carry, other_z=other_z):
+                    other_x = gx + dx_
+                    tell(it, (jnp.where(other_x >= gx_count, other_x - gx_count, other_x), other_z))
+                    return carry
+
+                lax.fori_loop(0 if dz_ else 1, gx_count, one, 0)
 
     def told(it):
         others = PK.at[it, pl.ds(0, total - 1)]
         pltpu.make_async_copy(others, others, pk_recv.at[it]).wait()
-        peaks = jnp.max(PK[it], axis=0)
-        step = 0.125 / jnp.max(peaks[1:2], axis=1, keepdims=True)
-        return step, jnp.max(peaks[0:1], axis=1, keepdims=True)
+        PEAKS[it] = jnp.max(PK[it], axis=0)
 
     def tell_sent():
         others = PK.at[0, pl.ds(0, total - 1)]
@@ -567,8 +601,8 @@
                 pltpu.make_async_remote_copy(
                     src_ref=CE.at[number],
                     dst_ref=CH.at[there],
-                    send_sem=send_sem.at[(2, 3, 6, 7)[number]],
-                    recv_sem=recv_sem.at[10 + number],
+                    send_sem=send_sem.at[corner_sent[number]],
+                    recv_sem=recv_sem.at[slot(5) + (number if z_sides == 2 else number // 2)],
                     device_id=target[a + b],
                     device_id_type=MESH,
                 ),
@@ -670,11 +704,11 @@
 
         lax.fori_loop(0, inside // size, inside_trial, 0)
 
-    step, top = told(0)
-    tell_sent()
-    tops = [top]
-
-    def second_stress(x, size):
+    def first_step():
+        told(0)
+        return step_of(PEAKS[0])
+
+    def second_stress(step, x, size):
         here = pl.ds(x, size)
         pres = PIN[here] - step * DV[here]
         PR[here] = pres
@@ -684,45 +718,66 @@
         )
 
     lowest = jnp.full((nz, ny), -jnp.inf, jnp.float32)
-    most = (lowest, lowest)
-    if inside > 0:
-
-        def inside_stress(i, most):
-            f, eta = second_stress(2 + i * size, size)
-            return jnp.maximum(most[0], f), jnp.maximum(most[1], eta)
-
-        most = lax.fori_loop(0, inside // size, inside_stress, most)
-    MOST[2, 0], MOST[2, 1] = most
-
-    wait_got(x_copies)
-    wait_got(corner_copies)
-    for number, side, row in ((0, "xl", 0), (1, "xh", rows - 1)):
-        sign = 0.5 - number
-        beyond = row + 2 * number
-        for c in range(3):
-            RF[c, row + 1] = RF[c, row + 1] - sign * XH[number, c]
-
-        @pl.when(has[side])
-        def _(number=number, sign=sign, row=row, beyond=beyond):
-            sub = lax.broadcasted_iota(jnp.int32, (nz, ny), 0)
+
+    def inside_rows(step):
+        most = (lowest, lowest)
+        if inside > 0:
+
+            def inside_stress(i, most):
+                f, eta = second_stress(step, 2 + i * size, size)
+                return jnp.maximum(most[0], f), jnp.maximum(most[1], eta)
+
+            most = lax.fori_loop(0, inside // size, inside_stress, most)
+        MOST[2, 0], MOST[2, 1] = most
+
+    def end_trials():
+        wait_got(x_copies)
+        wait_got(corner_copies)
+        for number, side, row in ((0, "xl", 0), (1, "xh", rows - 1)):
+            sign = 0.5 - number
+            beyond = row + 2 * number
             for c in range(3):
-                low = jnp.where(sub == 0, jnp.broadcast_to(CH[2 * number, 3 + c], (nz, ny)), 0.0)
-                high = jnp.where(sub == nz - 1, jnp.broadcast_to(CH[2 * number + 1, 3 + c], (nz, ny)), 0.0)
-                RF[c, beyond] = XH[number, 3 + c] + sign * SX[0, c, row + 1] + 0.5 * (high - low)
-
-        for layer in range(2):
-            for c in range(3):
-                RZF[layer, c, row] = RZF[layer, c, row] - sign * CH[2 * number + layer, c]
-    if inside > 0:
-        second_trial(0, 2)
-        second_trial(rows - 2, 2)
-    else:
-        second_trial(0, rows)
-
-    for i, x in enumerate((0, rows - 2) if inside > 0 else (0,)):
-        MOST[i, 0], MOST[i, 1] = second_stress(x, 2 if inside > 0 else rows)
-    if inside <= 0:
-        MOST[1, 0], MOST[1, 1] = lowest, lowest
+                RF[c, row + 1] = RF[c, row + 1] - sign * XH[number, c]
+
+            @pl.when(has[side])
+            def _(number=number, sign=sign, row=row, beyond=beyond):
+                sub = lax.broadcasted_iota(jnp.int32, (nz, ny), 0)
+                for c in range(3):
+                    low = jnp.where(sub == 0, jnp.broadcast_to(CH[2 * number, 3 + c], (nz, ny)), 0.0)
+                    high = jnp.where(sub == nz - 1, jnp.broadcast_to(CH[2 * number + 1, 3 + c], (nz, ny)), 0.0)
+                    RF[c, beyond] = XH[number, 3 + c] + sign * SX[0, c, row + 1] + 0.5 * (high - low)
+
+            for layer in range(2):
+                for c in range(3):
+                    RZF[layer, c, row] = RZF[layer, c, row] - sign * CH[2 * number + layer, c]
+        if inside > 0:
+            second_trial(0, 2)
+            second_trial(rows - 2, 2)
+        else:
+            second_trial(0, rows)
+
+    def end_rows(step):
+        for i, x in enumerate((0, rows - 2) if inside > 0 else (0,)):
+            MOST[i, 0], MOST[i, 1] = second_stress(step, x, 2 if inside > 0 else rows)
+        if inside <= 0:
+            MOST[1, 0], MOST[1, 1] = lowest, lowest
+
+    @pl.when(jnp.logical_not(has["xh"]))
+    def _():
+        step = first_step()
+        inside_rows(step)
+        end_trials()
+        end_rows(step)
+
+    @pl.when(has["xh"])
+    def _():
+        end_trials()
+        step = first_step()
+        inside_rows(step)
+        end_rows(step)
+
+    tell_sent()
+    step = step_of(PEAKS[0])
     tell_all(1)
     wait_sent(corner_copies)
     sx_copies = [
@@ -730,7 +785,6 @@
         ("xl", described("xl", SX.at[1, :, pl.ds(1, 1)], XHL.at[1], 2, 3)),
     ]
     start(sx_copies[1:])
-    start(sx_copies[:1])
     sz_copies = [
         ("zh", described("zh", SEL.at[1], ZHL.at[0], 1, 1)),
         ("zl", described("zl", SEL.at[0], ZHL.at[1], 1, 1)),
@@ -739,11 +793,12 @@
 
     def moved(x, carry):
         for c in range(3):
-            V[c, at(x + 1)] = V[c, at(x + 1)] + step * RF[c, at(x + 1)]
+            MOVED[c, at(x)] = V[c, at(x + 1)] + step * RF[c, at(x + 1)]
         return carry
 
     over_rows(moved)
     wait_got(sz_copies)
+    start(sx_copies[:1])
 
     def last_force(x, carry):
         def diff_z(c, f):
@@ -751,33 +806,35 @@
 
         force = forces(1, x, block, diff_z)
         for c in range(3):
-            RF[c, at(x + 1)] = force[c]
+            FORCE[c, at(x)] = force[c]
         return carry
 
     over_rows(last_force)
     wait_got(sx_copies)
     for c in range(3):
-        RF[c, 1] = RF[c, 1] - 0.5 * XHL[0, c, 0]
-        RF[c, rows] = RF[c, rows] + 0.5 * XHL[1, c, 0]
-    step, top = told(1)
-    tops.append(top)
-
-    def last_velocity(x, carry):
-        for c in range(3):
-            VOUT[c, at(x)] = V[c, at(x + 1)] + step * RF[c, at(x + 1)]
-        return carry
-
-    over_rows(last_velocity)
-    peak_out[...] = jnp.concatenate(tops, axis=1)[0]
+        FORCE[c, 0] = FORCE[c, 0] - 0.5 * XHL[0, c, 0]
+        FORCE[c, rows - 1] = FORCE[c, rows - 1] + 0.5 * XHL[1, c, 0]
+    told(1)
     wait_sent(x_copies + z_copies + sx_copies + sz_copies)
     tell_sent()
 
 
-def store_kernel(*refs):
-    held, out, sem = refs[:5], refs[5:10], refs[10]
-    copies = [pltpu.make_async_copy(a, b, sem.at[i]) for i, (a, b) in enumerate(zip(held, out))]
-    for copy in copies:
+def store_kernel(moved, pres, tau, plas, force, peaks, v_out, p_out, t_out, l_out, top_out, V, TOP, sem):
+    copies = [
+        pltpu.make_async_copy(source, place, sem.at[i])
+        for i, (source, place) in enumerate(
+            ((tau, t_out), (pres, p_out), (plas, l_out), (V, v_out), (TOP, top_out))
+        )
+    ]
+    for copy in copies[:3]:
         copy.start()
+    step = step_of(peaks[ITERS - 1])
+    for c in range(3):
+        V[c] = moved[c] + step * force[c]
+    copies[3].start()
+    tops = [top_of(peaks[it]) for it in range(ITERS)]
+    TOP[...] = jnp.concatenate(tops, axis=1)[0]
+    copies[4].start()
     for copy in copies:
         copy.wait()
 
@@ -793,12 +850,15 @@
         vm = lambda *shape: pltpu.VMEM(shape, f32)
         hops = len(bits_of(gx_count)) + len(bits_of(gz_count // 2))
         anywhere = pl.BlockSpec(memory_space=pl.ANY)
+        within = pl.BlockSpec(memory_space=pltpu.VMEM)
+        half = ny // 2 if ny % 256 == 0 else ny
         shapes = (velocity.shape, pressure.shape, stress_old.shape, plastic.shape)
+        inner = (velocity.shape, (ITERS, 1, half))
         held = pl.pallas_call(
             functools.partial(kernel, gx_count, gz_count),
-            out_shape=tuple(vm(*shape) for shape in shapes + ((ITERS,),)),
+            out_shape=tuple(vm(*shape) for shape in shapes + inner),
             in_specs=[anywhere] * 6,
-            out_specs=(pl.BlockSpec(memory_space=pltpu.VMEM),) * 5,
+            out_specs=(within,) * 6,
             scratch_shapes=[
                 vm(3, rows + 2, nz, ny),
                 vm(8, *cells),
@@ -831,10 +891,10 @@
                 vm(*cells),
                 vm(*cells),
                 vm(3, 2, nz, ny),
-                vm(ITERS, total, 2, ny // 2 if ny % 256 == 0 else ny),
+                vm(ITERS, total, 1, half),
                 pltpu.SemaphoreType.DMA,
-                pltpu.SemaphoreType.DMA((8,)),
-                pltpu.SemaphoreType.DMA((14,)),
+                pltpu.SemaphoreType.DMA((sems_of(sides_of(gz_count))[0],)),
+                pltpu.SemaphoreType.DMA((sems_of(sides_of(gz_count))[1],)),
                 pltpu.SemaphoreType.DMA,
                 pltpu.SemaphoreType.DMA((ITERS,)),
                 pltpu.SemaphoreType.REGULAR,
@@ -847,9 +907,9 @@
             store_kernel,
             out_shape=tuple(jax.ShapeDtypeStruct(shape, f32) for shape in shapes)
             + (jax.ShapeDtypeStruct((ITERS,), f32),),
-            in_specs=[anywhere] * 5,
+            in_specs=[within, anywhere, anywhere, anywhere, within, within],
             out_specs=(anywhere,) * 5,
-            scratch_shapes=[pltpu.SemaphoreType.DMA((5,))],
+            scratch_shapes=[vm(*velocity.shape), vm(ITERS), pltpu.SemaphoreType.DMA((5,))],
         )(*held)
 
     in_specs = (

time: 21.7 us -> 21.6 us (level)
  no operation moved by 1% of the time
where the time goes in v5:
time: 21.6 us; the launch traced here: 21.4 us
  Pallas kernels  20.8 us (96%)
  between operations  0.64 us (3%)
    pallas_call x1, Pallas kernels, per_device(): pl.pallas_call(functools.partial(kernel, gx_count, gz_count), out_shape=t...  19.6 us
    pallas_call x1, Pallas kernels, per_device(): pl.pallas_call(store_kernel, out_shape=tuple((jax.ShapeDtypeStruct(shape,...  1.14 us

profile of v5, /device:TPU:0, one launch (start us, length us, event | category | flops | bytes accessed | tf_op | source)
XLA Modules:
  0.0 21.4 jit_solution(924395417550458361)
XLA Ops:
  0.6 19.6 %shard_map.101 = (f32[3,16,8,256]{3,2,1,0:T(8,128)S(1)}, f32[16,8,256]{2,1,0:T(8,128)S(1)}, f32[6,16,8,256]{3,2,1,0:T(8,128)S(1)}, f32[16,8,256]{2,1,0:T(8,128)S...) custom-call(f32[3,16,8,256]{3,2,1,0:T(8,128)} %vel_in.1, f32[16,8,256]{2,1,0:T(8,128)} %pres_in.1, ...), custom_call_target="tpu_custom_call" | custom-call | tf_op jit(solution)/shard_map/pallas_call | solution.py:857
  20.3 1.1 %shard_map.102 = (f32[3,16,8,256]{3,2,1,0:T(8,128)}, f32[16,8,256]{2,1,0:T(8,128)}, f32[6,16,8,256]{3,2,1,0:T(8,128)}, f32[16,8,256]{2,1,0:T(8,128)}, f32[2]{0:T(128)}) custom-call(f32[3,16,8,256]{3,2,1,0:T(8,128)S(1)} %get-tuple-element.11.moved, f32[16,8,256]{2,1,0:T(8,128)S(1)} %get-tuple-element.12.pres, f32[6,16,8,256]{3,2,1,0:T(8,128)S(1)} %get-tuple-element.13.tau, ...), custom_call_target="tpu_custom_call" | custom-call | tf_op jit(solution)/shard_map/pallas_call | solution.py:906

commit v6 on v5

--- a/solution.py
+++ b/solution.py
@@ -175,6 +175,7 @@
             signal(barrier, (gx, gz + 1))
 
     plas_load.start()
+    vel_load.start()
 
     @pl.when(odd)
     def _():
@@ -269,7 +270,6 @@
         ("zl", described("zl", plas_in, PZH.at[1], 0, 0)),
     ]
     start(pz_copies)
-    vel_load.start()
     for copy in rest_loads:
         copy.start()
     weak_load.start()
@@ -293,6 +293,7 @@
         zero(SX.at[it, :, pl.ds(0, 1)])
         zero(SX.at[it, :, pl.ds(rows + 1, 1)])
 
+    vel_load.wait()
     @pl.when(odd)
     def _():
         greeters = 2 * (one_if(has["xl"]) + one_if(has["xh"]))
@@ -306,8 +307,8 @@
         pl.semaphore_wait(pair_sem, 1)
 
     vel_copies = [
-        ("xh", described("xh", vel_in.at[:, pl.ds(rows - 1, 1)], V.at[:, pl.ds(0, 1)], 2, 2)),
-        ("xl", described("xl", vel_in.at[:, pl.ds(0, 1)], V.at[:, pl.ds(rows + 1, 1)], 2, 2)),
+        ("xh", described("xh", V.at[:, pl.ds(rows, 1)], V.at[:, pl.ds(0, 1)], 2, 2)),
+        ("xl", described("xl", V.at[:, pl.ds(1, 1)], V.at[:, pl.ds(rows + 1, 1)], 2, 2)),
     ]
     start_far(vel_copies)
 
@@ -347,8 +348,6 @@
 
     def at(x):
         return pl.ds(x, block)
-
-    vel_load.wait()
 
     def vel_edges(x, carry):
         for c in range(3):
@@ -609,17 +608,8 @@
             )
         )
 
-    def one_side(number, far):
+    def one_edge(number, far):
         row = (rows - 1) * number
-        wait_got(plas_copies[number : number + 1])
-        for beside in range(min(REACH, block)):
-            here = beside if number == 0 else rows - 1 - beside
-            sum_ = SM[here]
-            for k in range(beside + 1, REACH + 1):
-                place = REACH + beside - k if number == 0 else k - 1 - beside
-                sum_ = sum_ + gauss_weights[REACH + k] * GXH[number, place]
-            SM[here] = sum_
-        MOST[number, 0], MOST[number, 1] = first_stress(number * block)
         force = forces(0, row, 1, lambda c, f: dz_inside(f))
         for c in range(3):
             XS[number, c] = SX[0, c, row + 1]
@@ -632,7 +622,20 @@
                 CE[where, 3 + c] = SE[layer, c, row]
         if far:
             wait_sent(vel_copies)
-            start(x_copies[1 - number : 2 - number])
+        start(x_copies[1 - number : 2 - number])
+
+    def one_side(number, far):
+        wait_got(plas_copies[number : number + 1])
+        for beside in range(min(REACH, block)):
+            here = beside if number == 0 else rows - 1 - beside
+            sum_ = SM[here]
+            for k in range(beside + 1, REACH + 1):
+                place = REACH + beside - k if number == 0 else k - 1 - beside
+                sum_ = sum_ + gauss_weights[REACH + k] * GXH[number, place]
+            SM[here] = sum_
+        MOST[number, 0], MOST[number, 1] = first_stress(number * block)
+        if far:
+            one_edge(number, far)
         if far:
             if len(rounds) > 1:
                 hop_wait(len(rounds) - 1)
@@ -647,7 +650,12 @@
         pl.semaphore_wait(pair_sem, 1)
 
     tell_all(0)
-    start_near(x_copies)
+    for place, number in ((gx_odd, 0), (gx_even, 1)):
+
+        @pl.when(place)
+        def _(number=number):
+            one_edge(number, False)
+
     wait_sent(vz_copies)
     wait_sent(plas_copies)
     start(corner_copies)
@@ -762,14 +770,14 @@
         if inside <= 0:
             MOST[1, 0], MOST[1, 1] = lowest, lowest
 
-    @pl.when(jnp.logical_not(has["xh"]))
+    @pl.when(gx >= gx_count // 2)
     def _():
         step = first_step()
         inside_rows(step)
         end_trials()
         end_rows(step)
 
-    @pl.when(has["xh"])
+    @pl.when(gx < gx_count // 2)
     def _():
         end_trials()
         step = first_step()

time: 21.6 us -> 21.3 us (0.986)
  Pallas kernels: 20.8 us -> 20.5 us
    pallas_call x1, Pallas kernels: 19.6 us -> 19.4 us  [per_device(): pl.pallas_call(functools.partial(kernel, gx_count, gz_count), out_shape=t...]
where the time goes in v6:
time: 21.3 us; the launch traced here: 21.2 us
  Pallas kernels  20.5 us (96%)
  between operations  0.64 us (3%)
    pallas_call x1, Pallas kernels, per_device(): pl.pallas_call(functools.partial(kernel, gx_count, gz_count), out_shape=t...  19.4 us
    pallas_call x1, Pallas kernels, per_device(): pl.pallas_call(store_kernel, out_shape=tuple((jax.ShapeDtypeStruct(shape,...  1.14 us

profile of v6, /device:TPU:0, one launch (start us, length us, event | category | flops | bytes accessed | tf_op | source)
XLA Modules:
  0.0 21.2 jit_solution(9557325085410645932)
XLA Ops:
  0.6 19.4 %shard_map.101 = (f32[3,16,8,256]{3,2,1,0:T(8,128)S(1)}, f32[16,8,256]{2,1,0:T(8,128)S(1)}, f32[6,16,8,256]{3,2,1,0:T(8,128)S(1)}, f32[16,8,256]{2,1,0:T(8,128)S...) custom-call(f32[3,16,8,256]{3,2,1,0:T(8,128)} %vel_in.1, f32[16,8,256]{2,1,0:T(8,128)} %pres_in.1, ...), custom_call_target="tpu_custom_call" | custom-call | tf_op jit(solution)/shard_map/pallas_call | solution.py:865
  20.0 1.1 %shard_map.102 = (f32[3,16,8,256]{3,2,1,0:T(8,128)}, f32[16,8,256]{2,1,0:T(8,128)}, f32[6,16,8,256]{3,2,1,0:T(8,128)}, f32[16,8,256]{2,1,0:T(8,128)}, f32[2]{0:T(128)}) custom-call(f32[3,16,8,256]{3,2,1,0:T(8,128)S(1)} %get-tuple-element.11.moved, f32[16,8,256]{2,1,0:T(8,128)S(1)} %get-tuple-element.12.pres, f32[6,16,8,256]{3,2,1,0:T(8,128)S(1)} %get-tuple-element.13.tau, ...), custom_call_target="tpu_custom_call" | custom-call | tf_op jit(solution)/shard_map/pallas_call | solution.py:914
